TPU v7x, 32 devices: a whole 2x2x4 slice. The times are simulated.
32 devices in a mesh: seq: 4 (over y, x), fsdp: 8 (over z, core).
Axes of the slice: x: 2, y: 2, z: 4, core: 2. Of those that a mesh axis runs over, the one named last changes fastest.
Arguments:
- images: bfloat16 [24, 512, 1152], P('fsdp', 'seq'), may hold values from -6 to 6
- key_mask: int32 [24, 512], P('fsdp'), may hold values from 0 to 1, as said below
- attn_gain: bfloat16 [1152], P('fsdp'), may hold values from 0.25 to 1.75
- attn_shift: bfloat16 [1152], P('fsdp'), may hold values from -3 to 3
- query_weight: bfloat16 [1152, 1152], P('fsdp'), may hold values from -0.1875 to 0.1875
- key_weight: bfloat16 [1152, 1152], P('fsdp'), may hold values from -0.1875 to 0.1875
- value_weight: bfloat16 [1152, 1152], P('fsdp'), may hold values from -0.1875 to 0.1875
- query_bias: bfloat16 [1152], P('fsdp'), may hold values from -3 to 3
- value_bias: bfloat16 [1152], P('fsdp'), may hold values from -0.1796875 to 0.1796875
- out_weight: bfloat16 [1152, 1152], P('fsdp'), may hold values from -1.5 to 1.5
- out_bias: bfloat16 [1152], P('fsdp'), may hold values from -3 to 3
- mlp_gain: bfloat16 [1152], P('fsdp'), may hold values from 0.25 to 1.75
- mlp_shift: bfloat16 [1152], P('fsdp'), may hold values from -3 to 3
- inner_weight: bfloat16 [1152, 4304], P('fsdp'), may hold values from -0.1875 to 0.1875
- inner_bias: bfloat16 [4304], P('fsdp'), may hold values from -3 to 3
- outer_weight: bfloat16 [4304, 1152], P('fsdp'), may hold values from -0.09375 to 0.09375
- outer_bias: bfloat16 [1152], P('fsdp'), may hold values from -3 to 3
- cotangent: bfloat16 [24, 512, 1152], P('fsdp', 'seq'), may hold values from -6 to 6
Outputs:
- layer_out: float32 [24, 512, 1152], P('fsdp', 'seq')
- images_grad: float32 [24, 512, 1152], P('fsdp', 'seq')
- attn_gain_grad: float32 [1152], P('fsdp')
- attn_shift_grad: float32 [1152], P('fsdp')
- query_weight_grad: float32 [1152, 1152], P('fsdp')
- key_weight_grad: float32 [1152, 1152], P('fsdp')
- value_weight_grad: float32 [1152, 1152], P('fsdp')
- query_bias_grad: float32 [1152], P('fsdp')
- value_bias_grad: float32 [1152], P('fsdp')
- out_weight_grad: float32 [1152, 1152], P('fsdp')
- out_bias_grad: float32 [1152], P('fsdp')
- mlp_gain_grad: float32 [1152], P('fsdp')
- mlp_shift_grad: float32 [1152], P('fsdp')
- inner_weight_grad: float32 [1152, 4304], P('fsdp')
- inner_bias_grad: float32 [4304], P('fsdp')
- outer_weight_grad: float32 [4304, 1152], P('fsdp')
- outer_bias_grad: float32 [1152], P('fsdp')
Inputs may be any that keep to these rules, and one draw needn't show every extreme that they name: `key_mask`: each image's row is 1 on its first positions and 0 after them; at least 128 positions are 1.
All inputs are finite; a program needn't handle non-finite values.
Results may differ from a plain program's by a relative error of at most 0.013.
The roundings to bfloat16 on the way count: a program that leaves them out, or rounds other values in their place, can miss the bound.
Values may be sent and summed in bfloat16 or wider, within the bound.
A program may use at most 256 MiB of HBM per device.

v0:
```python
import jax
import jax.numpy as jnp
from jax import lax
from jax.sharding import PartitionSpec as P

HD = 72


EPSILON = 1e-06
MASKED = -1e30


def product(left, right):
    return jnp.dot(left, right, preferred_element_type=jnp.float32)


def product_rows(left, right):
    return lax.dot_general(
        left, right, (((0,), (0,)), ((), ())), preferred_element_type=jnp.float32
    )


def product_back(left, right):
    return lax.dot_general(
        left, right, (((1,), (1,)), ((), ())), preferred_element_type=jnp.float32
    )


def gelu_tanh(values):
    return jax.nn.gelu(values, approximate=True)


def normalize(values):
    center = values - jnp.mean(values, axis=-1, keepdims=True)
    factor = lax.rsqrt(jnp.mean(center * center, axis=-1, keepdims=True) + EPSILON)
    return (center * factor, factor)


def norm_back(grad_normed, normed, factor):
    first = jnp.mean(grad_normed, axis=-1, keepdims=True)
    second = jnp.mean(grad_normed * normed, axis=-1, keepdims=True)
    return factor * (grad_normed - first - normed * second)


def forward_image(items):
    query, keys, values, valid = items
    length, local = query.shape
    heads = local // HD
    scale = HD ** (-0.5)
    block = min(512, length)
    key_three = keys.reshape(length, heads, HD)
    value_three = values.reshape(length, heads, HD)
    blocks = query.reshape(length // block, block, heads, HD)

    def forward_visit(query_block):
        scores = (
            jnp.einsum("qhd,khd->hqk", query_block, key_three, preferred_element_type=jnp.float32)
            * scale
        )
        scores = jnp.where(valid[None, None, :], scores, MASKED)
        highest = jnp.max(scores, axis=-1, keepdims=True)
        logsum = highest + jnp.log(jnp.sum(jnp.exp(scores - highest), axis=-1, keepdims=True))
        attention = jnp.exp(scores - logsum).astype(jnp.bfloat16)
        attended = jnp.einsum(
            "hqk,khd->qhd", attention, value_three, preferred_element_type=jnp.float32
        )
        return (attended.astype(jnp.bfloat16), logsum[..., 0])

    attended, logsum = lax.map(forward_visit, blocks)
    return (attended.reshape(length, local), logsum)


def backward_image(items):
    query, keys, values, attended, grad_out, logsum, valid = items
    length, local = query.shape
    heads = local // HD
    scale = HD ** (-0.5)
    block = min(512, length)
    count_blocks = length // block
    key_three = keys.reshape(length, heads, HD)
    value_three = values.reshape(length, heads, HD)
    blocks = (
        query.reshape(count_blocks, block, heads, HD),
        attended.reshape(count_blocks, block, heads, HD),
        grad_out.reshape(count_blocks, block, heads, HD),
        logsum,
    )
    zeros = jnp.zeros((length, heads, HD), jnp.float32)

    def backward_visit(carry, piece):
        query_block, out_block, grad_block, logsum_block = piece
        grad_keys, grad_values = carry
        scores = (
            jnp.einsum("qhd,khd->hqk", query_block, key_three, preferred_element_type=jnp.float32)
            * scale
        )
        scores = jnp.where(valid[None, None, :], scores, MASKED)
        chance = jnp.exp(scores - logsum_block[:, :, None])
        chance_low = chance.astype(jnp.bfloat16)
        grad_values = grad_values + jnp.einsum(
            "hqk,qhd->khd", chance_low, grad_block, preferred_element_type=jnp.float32
        )
        grad_chance = jnp.einsum(
            "qhd,khd->hqk", grad_block, value_three, preferred_element_type=jnp.float32
        )
        delta = jnp.sum(grad_block.astype(jnp.float32) * out_block.astype(jnp.float32), axis=-1).T
        grad_scores = (chance * (grad_chance - delta[:, :, None]) * scale).astype(jnp.bfloat16)
        grad_query = jnp.einsum(
            "hqk,khd->qhd", grad_scores, key_three, preferred_element_type=jnp.float32
        )
        grad_keys = grad_keys + jnp.einsum(
            "hqk,qhd->khd", grad_scores, query_block, preferred_element_type=jnp.float32
        )
        return ((grad_keys, grad_values), grad_query.astype(jnp.bfloat16))

    (grad_keys, grad_values), grad_query = lax.scan(backward_visit, (zeros, zeros), blocks)
    return (
        grad_query.reshape(length, local),
        grad_keys.astype(jnp.bfloat16).reshape(length, local),
        grad_values.astype(jnp.bfloat16).reshape(length, local),
    )


def shards(
    images,
    key_mask,
    attn_gain,
    attn_shift,
    query_weight,
    key_weight,
    value_weight,
    query_bias,
    value_bias,
    out_weight,
    out_bias,
    mlp_gain,
    mlp_shift,
    inner_weight,
    inner_bias,
    outer_weight,
    outer_bias,
    cotangent,
):
    gathered = (
        lax.all_gather(attn_gain, "fsdp", axis=0, tiled=True),
        lax.all_gather(attn_shift, "fsdp", axis=0, tiled=True),
        lax.all_gather(query_weight, "fsdp", axis=0, tiled=True),
        lax.all_gather(key_weight, "fsdp", axis=0, tiled=True),
        lax.all_gather(value_weight, "fsdp", axis=0, tiled=True),
        lax.all_gather(query_bias, "fsdp", axis=0, tiled=True),
        lax.all_gather(value_bias, "fsdp", axis=0, tiled=True),
        lax.all_gather(out_weight, "fsdp", axis=0, tiled=True),
        lax.all_gather(out_bias, "fsdp", axis=0, tiled=True),
        lax.all_gather(mlp_gain, "fsdp", axis=0, tiled=True),
        lax.all_gather(mlp_shift, "fsdp", axis=0, tiled=True),
        lax.all_gather(inner_weight, "fsdp", axis=0, tiled=True),
        lax.all_gather(inner_bias, "fsdp", axis=0, tiled=True),
        lax.all_gather(outer_weight, "fsdp", axis=0, tiled=True),
        lax.all_gather(outer_bias, "fsdp", axis=0, tiled=True),
    )
    (
        gain_attn,
        shift_attn,
        w_query,
        w_key,
        w_value,
        b_query,
        b_value,
        w_out,
        b_out,
        gain_mlp,
        shift_mlp,
        w_inner,
        b_inner,
        w_outer,
        b_outer,
    ) = gathered
    count, block_len, width = images.shape
    rows = count * block_len
    flat = images.reshape(rows, width).astype(jnp.float32)
    normed_one, factor_one = normalize(flat)
    hidden_one = (
        normed_one * gain_attn.astype(jnp.float32) + shift_attn.astype(jnp.float32)
    ).astype(jnp.bfloat16)
    query = (product(hidden_one, w_query) + b_query.astype(jnp.float32)).astype(jnp.bfloat16)
    keys = product(hidden_one, w_key).astype(jnp.bfloat16)
    values = (product(hidden_one, w_value) + b_value.astype(jnp.float32)).astype(jnp.bfloat16)
    query_heads, key_heads, value_heads = (
        lax.all_to_all(
            query.reshape(count, block_len, width), "seq", split_axis=2, concat_axis=1, tiled=True
        ),
        lax.all_to_all(
            keys.reshape(count, block_len, width), "seq", split_axis=2, concat_axis=1, tiled=True
        ),
        lax.all_to_all(
            values.reshape(count, block_len, width), "seq", split_axis=2, concat_axis=1, tiled=True
        ),
    )
    valid = key_mask > 0
    attended, logsum = lax.map(forward_image, (query_heads, key_heads, value_heads, valid))
    attended_tokens = lax.all_to_all(attended, "seq", split_axis=1, concat_axis=2, tiled=True)
    attended_flat = attended_tokens.reshape(rows, width)
    second = flat + product(attended_flat, w_out) + b_out.astype(jnp.float32)
    normed_two, factor_two = normalize(second)
    hidden_two = (normed_two * gain_mlp.astype(jnp.float32) + shift_mlp.astype(jnp.float32)).astype(
        jnp.bfloat16
    )
    inner = product(hidden_two, w_inner) + b_inner.astype(jnp.float32)
    active = gelu_tanh(inner).astype(jnp.bfloat16)
    layer_out = second + product(active, w_outer) + b_outer.astype(jnp.float32)
    unpacked = (
        lax.all_gather(attn_gain, "fsdp", axis=0, tiled=True),
        lax.all_gather(attn_shift, "fsdp", axis=0, tiled=True),
        lax.all_gather(query_weight, "fsdp", axis=0, tiled=True),
        lax.all_gather(key_weight, "fsdp", axis=0, tiled=True),
        lax.all_gather(value_weight, "fsdp", axis=0, tiled=True),
        lax.all_gather(query_bias, "fsdp", axis=0, tiled=True),
        lax.all_gather(value_bias, "fsdp", axis=0, tiled=True),
        lax.all_gather(out_weight, "fsdp", axis=0, tiled=True),
        lax.all_gather(out_bias, "fsdp", axis=0, tiled=True),
        lax.all_gather(mlp_gain, "fsdp", axis=0, tiled=True),
        lax.all_gather(mlp_shift, "fsdp", axis=0, tiled=True),
        lax.all_gather(inner_weight, "fsdp", axis=0, tiled=True),
        lax.all_gather(inner_bias, "fsdp", axis=0, tiled=True),
        lax.all_gather(outer_weight, "fsdp", axis=0, tiled=True),
        lax.all_gather(outer_bias, "fsdp", axis=0, tiled=True),
    )
    (
        gain_attn,
        shift_attn,
        w_query,
        w_key,
        w_value,
        b_query,
        b_value,
        w_out,
        b_out,
        gain_mlp,
        shift_mlp,
        w_inner,
        b_inner,
        w_outer,
        b_outer,
    ) = unpacked
    upstream = cotangent.reshape(rows, width)
    grad_active = product_back(upstream, w_outer)
    grad_inner = jax.vjp(gelu_tanh, inner)[1](grad_active)[0]
    grad_inner_low = grad_inner.astype(jnp.bfloat16)
    grad_hidden_two = product_back(grad_inner_low, w_inner)
    grad_second = upstream.astype(jnp.float32) + norm_back(
        grad_hidden_two * gain_mlp.astype(jnp.float32), normed_two, factor_two
    )
    mlp_terms = (
        jnp.sum(grad_hidden_two * normed_two, axis=0),
        jnp.sum(grad_hidden_two, axis=0),
        product_rows(hidden_two, grad_inner_low),
        jnp.sum(grad_inner, axis=0),
        product_rows(active, upstream),
        jnp.sum(upstream.astype(jnp.float32), axis=0),
    )
    grad_second_low = grad_second.astype(jnp.bfloat16)
    grad_attended = product_back(grad_second_low, w_out).astype(jnp.bfloat16)
    grad_heads = lax.all_to_all(
        grad_attended.reshape(count, block_len, width),
        "seq",
        split_axis=2,
        concat_axis=1,
        tiled=True,
    )
    grad_query_heads, grad_key_heads, grad_value_heads = lax.map(
        backward_image, (query_heads, key_heads, value_heads, attended, grad_heads, logsum, valid)
    )
    grad_query, grad_keys, grad_values = (
        lax.all_to_all(grad_query_heads, "seq", split_axis=1, concat_axis=2, tiled=True),
        lax.all_to_all(grad_key_heads, "seq", split_axis=1, concat_axis=2, tiled=True),
        lax.all_to_all(grad_value_heads, "seq", split_axis=1, concat_axis=2, tiled=True),
    )
    grad_query = grad_query.reshape(rows, width)
    grad_keys = grad_keys.reshape(rows, width)
    grad_values = grad_values.reshape(rows, width)
    grad_hidden_one = (
        product_back(grad_query, w_query)
        + product_back(grad_keys, w_key)
        + product_back(grad_values, w_value)
    )
    images_grad = grad_second + norm_back(
        grad_hidden_one * gain_attn.astype(jnp.float32), normed_one, factor_one
    )
    attn_terms = (
        jnp.sum(grad_hidden_one * normed_one, axis=0),
        jnp.sum(grad_hidden_one, axis=0),
        product_rows(hidden_one, grad_query),
        product_rows(hidden_one, grad_keys),
        product_rows(hidden_one, grad_values),
        jnp.sum(grad_query.astype(jnp.float32), axis=0),
        jnp.sum(grad_values.astype(jnp.float32), axis=0),
        product_rows(attended_flat, grad_second_low),
        jnp.sum(grad_second, axis=0),
    )
    shard_grads = (
        lax.psum_scatter(attn_terms[0], "fsdp", scatter_dimension=0, tiled=True),
        lax.psum_scatter(attn_terms[1], "fsdp", scatter_dimension=0, tiled=True),
        lax.psum_scatter(attn_terms[2], "fsdp", scatter_dimension=0, tiled=True),
        lax.psum_scatter(attn_terms[3], "fsdp", scatter_dimension=0, tiled=True),
        lax.psum_scatter(attn_terms[4], "fsdp", scatter_dimension=0, tiled=True),
        lax.psum_scatter(attn_terms[5], "fsdp", scatter_dimension=0, tiled=True),
        lax.psum_scatter(attn_terms[6], "fsdp", scatter_dimension=0, tiled=True),
        lax.psum_scatter(attn_terms[7], "fsdp", scatter_dimension=0, tiled=True),
        lax.psum_scatter(attn_terms[8], "fsdp", scatter_dimension=0, tiled=True),
        lax.psum_scatter(mlp_terms[0], "fsdp", scatter_dimension=0, tiled=True),
        lax.psum_scatter(mlp_terms[1], "fsdp", scatter_dimension=0, tiled=True),
        lax.psum_scatter(mlp_terms[2], "fsdp", scatter_dimension=0, tiled=True),
        lax.psum_scatter(mlp_terms[3], "fsdp", scatter_dimension=0, tiled=True),
        lax.psum_scatter(mlp_terms[4], "fsdp", scatter_dimension=0, tiled=True),
        lax.psum_scatter(mlp_terms[5], "fsdp", scatter_dimension=0, tiled=True),
    )
    summed = lax.psum(
        (
            shard_grads[0],
            shard_grads[1],
            shard_grads[2],
            shard_grads[3],
            shard_grads[4],
            shard_grads[5],
            shard_grads[6],
            shard_grads[7],
            shard_grads[8],
            shard_grads[9],
            shard_grads[10],
            shard_grads[11],
            shard_grads[12],
            shard_grads[13],
            shard_grads[14],
        ),
        "seq",
    )
    return (
        layer_out.reshape(count, block_len, width),
        images_grad.reshape(count, block_len, width),
        summed[0],
        summed[1],
        summed[2],
        summed[3],
        summed[4],
        summed[5],
        summed[6],
        summed[7],
        summed[8],
        summed[9],
        summed[10],
        summed[11],
        summed[12],
        summed[13],
        summed[14],
    )


def solution(mesh):
    placed = (
        P("fsdp", "seq", None),
        P("fsdp", None),
        P("fsdp"),
        P("fsdp"),
        P("fsdp", None),
        P("fsdp", None),
        P("fsdp", None),
        P("fsdp"),
        P("fsdp"),
        P("fsdp", None),
        P("fsdp"),
        P("fsdp"),
        P("fsdp"),
        P("fsdp", None),
        P("fsdp"),
        P("fsdp", None),
        P("fsdp"),
        P("fsdp", "seq", None),
    )
    return jax.shard_map(
        shards,
        mesh=mesh,
        in_specs=placed,
        out_specs=(
            P("fsdp", "seq", None),
            P("fsdp", "seq", None),
            P("fsdp"),
            P("fsdp"),
            P("fsdp", None),
            P("fsdp", None),
            P("fsdp", None),
            P("fsdp"),
            P("fsdp"),
            P("fsdp", None),
            P("fsdp"),
            P("fsdp"),
            P("fsdp"),
            P("fsdp", None),
            P("fsdp"),
            P("fsdp", None),
            P("fsdp"),
        ),
        check_vma=False,
    )
```

profile of v0, /device:TPU:0, one launch (start us, length us, event | category | flops | bytes accessed | tf_op | source)
XLA Modules:
  0.0 1205.4 jit_solution(2965813202933017199)
XLA Ops:
  15.5 33.4 %all-reduce.23 = (bf16[1152]{0:T(1024)(128)(2,1)S(1)}, bf16[1152]{0:T(1024)(128)(2,1)S(1)}, bf16[1152]{0:T(1024)(128)(2,1)S(1)}, bf16[1152]{0:T(1024)(128)(2,1)S...) all-reduce(bf16[1152]{0:T(1024)(128)(2,1)S(1)} %dynamic-update-slic, ...), channel_id=1, replica_groups=mesh['seq'=4,'fsdp'=8] {'fsdp'}, use_global_device_ids=true, to_apply=%add.1 | all-reduce | flops 13520 | bytes 54080
  60.2 22.2 %all-gather.12.cloned.1.call-done = bf16[1152,1152]{1,0:T(8,128)(2,1)} async-done(((bf16[144,1152]{1,0:T(8,128)(2,1)}), bf16[1152,1152]{1,0:T(8,128)(2,1)}) %all-gather.12.cloned.1.call-update) | async-done | bytes 2654224 | tf_op jit(solution)/shard_map/all_gather | solution.py:148
  93.3 23.8 %all-gather.10.cloned.1.call-done = bf16[1152,1152]{1,0:T(8,128)(2,1)} async-done(((bf16[144,1152]{1,0:T(8,128)(2,1)}), bf16[1152,1152]{1,0:T(8,128)(2,1)}) %all-gather.10.cloned.1.call-update) | async-done | bytes 2654224 | tf_op jit(solution)/shard_map/all_gather | solution.py:147
  117.2 4.4 fusion.26
  124.8 4.5 all-to-all-start.1
  130.6 14.4 %all-to-all-done.1 = bf16[3,128,1152]{1,0,2:T(4,128)(2,1)} async-done(((bf16[3,128,1152]{1,0,2:T(4,128)(2,1)}), bf16[3,128,1152]{1,0,2:T(4,128)(2,1)}, u32[]{:S(2)}, u32[]{:S(2)}) %all-to-all-start.1) | async-done | bytes 884768 | tf_op jit(solution)/shard_map/all_to_all | solution.py:189
  147.7 13.9 %while.10 = (s32[]{:T(128)}, bf16[3,512,288]{1,2,0:T(8,128)(2,1)}, f32[3,1,4,512]{3,2,1,0:T(4,128)}, bf16[3,512,288]{1,2,0:T(8,128)(2,1)S(1)}, pred[3,512]{1,0:T...) while((s32[]{:T(128)}, bf16[3,512,288]{1,2,0:T(8,128)(2,1)}, ...), condition=%wide.region_5.6_spmd, body=%wide.region_2.5_spmd.sunk | while | flops 313669632 | bytes 16190065 | solution.py:200
  165.0 4.3 all-to-all-start.3
  173.3 15.2 %all-to-all-done.3 = bf16[3,512,288]{2,0,1:T(4,128)(2,1)} async-done(((bf16[3,512,288]{2,0,1:T(4,128)(2,1)}), bf16[3,512,288]{2,0,1:T(4,128)(2,1)}, u32[]{:S(2)}, u32[]{:S(2)}) %all-to-all-start.3) | async-done | bytes 884768 | tf_op jit(solution)/shard_map/all_to_all | solution.py:201
  200.5 47.5 %all-gather.18.cloned.1.call-done = bf16[8,538,1152]{2,1,0:T(8,128)(2,1)} async-done(((bf16[1,538,1152]{2,1,0:T(8,128)(2,1)}), bf16[8,538,1152]{2,1,0:T(8,128)(2,1)}) %all-gather.18.cloned.1.call-update) | async-done | bytes 9916432 | tf_op jit(solution)/shard_map/all_gather | solution.py:158
  248.0 12.4 %reshape.318 = bf16[4304,1152]{1,0:T(8,128)(2,1)} reshape(bf16[8,538,1152]{2,1,0:T(8,128)(2,1)} %all-gather.18.cloned.1.call-done) | data formatting | bytes 19832832
  260.4 10.5 fusion.44
  270.9 72.6 %all-gather.16.cloned.1.call-done = bf16[1152,4304]{1,0:T(8,128)(2,1)} async-done(((bf16[144,4304]{1,0:T(8,128)(2,1)}), bf16[1152,4304]{1,0:T(8,128)(2,1)}) %all-gather.16.cloned.1.call-update) | async-done | bytes 9916432 | tf_op jit(solution)/shard_map/all_gather | solution.py:156
  343.5 20.9 %fusion.38 = (f32[4304]{0:T(1024)}, bf16[384,4304]{0,1:T(8,128)(2,1)S(1)}, f32[384,4304]{0,1:T(8,128)}) fusion(f32[384,4304]{0,1:T(8,128)} %fusion.44, f32[4304]{0:T(1024)} %convert_element_type.163, bf16[1152,4304]{1,0:T(8,128)(2,1)} %all-gather.16.cloned.1.call-done, f32[384,1152]{1,0:T(8,128)} %copy-done.1, f32[1152]{0:T(1024)} %convert_element_type.161, ...), kind=kOutput, calls=%fused_computation.108 | convolution fusion | flops 3846471424 | bytes 28259968 | tf_op jit(solution)/shard_map/dot_general | solution.py:14
  364.4 10.7 multiply_reduce_fusion
  381.7 4.7 convolution_convert_fusion.2
  389.6 19.9 %all_to_all.132 = bf16[3,128,1152]{1,0,2:T(4,128)(2,1)S(1)} all-to-all(bf16[3,128,1152]{1,0,2:T(4,128)(2,1)} %copy.74), channel_id=1, replica_groups=mesh['seq'=4,'fsdp'=8] {'seq'}, dimensions={2} | all-to-all | bytes 1769472 | tf_op jit(solution)/shard_map/all_to_all | solution.py:263
  413.7 27.9 %while.27 = (s32[]{:T(128)}, bf16[3,512,288]{1,2,0:T(8,128)(2,1)}, bf16[3,512,288]{1,2,0:T(8,128)(2,1)}, bf16[3,512,288]{1,2,0:T(8,128)(2,1)}, bf16[3,512,288]{1...) while((s32[]{:T(128)}, bf16[3,512,288]{1,2,0:T(8,128)(2,1)}, ...), condition=%wide.region_12.13_spmd, body=%wide.region_10.12_spmd.sunk | while | flops 767539200 | bytes 27183264 | solution.py:270
  449.0 18.1 %all-to-all-done.5 = bf16[3,512,288]{2,0,1:T(4,128)(2,1)S(1)} async-done(((bf16[3,512,288]{2,0,1:T(4,128)(2,1)}), bf16[3,512,288]{2,0,1:T(4,128)(2,1)S(1)}, u32[]{:S(2)}, u32[]{:S(2)}) %all-to-all-start.5) | async-done | bytes 884768 | tf_op jit(solution)/shard_map/all_to_all | solution.py:274
  478.9 21.9 %all_to_all.133 = bf16[3,512,288]{2,0,1:T(4,128)(2,1)S(1)} all-to-all(bf16[3,512,288]{2,0,1:T(4,128)(2,1)S(1)} %copy.79), channel_id=1, replica_groups=mesh['seq'=4,'fsdp'=8] {'seq'}, dimensions={1} | all-to-all | bytes 1769472 | tf_op jit(solution)/shard_map/all_to_all | solution.py:275
  503.7 5.2 fusion.47
  511.8 20.5 %all_to_all.134 = bf16[3,512,288]{2,0,1:T(4,128)(2,1)S(1)} all-to-all(bf16[3,512,288]{2,0,1:T(4,128)(2,1)S(1)} %copy.81), channel_id=1, replica_groups=mesh['seq'=4,'fsdp'=8] {'seq'}, dimensions={1} | all-to-all | bytes 1769472 | tf_op jit(solution)/shard_map/all_to_all | solution.py:276
  535.8 5.2 fusion.48
  542.5 11.6 fusion.28
  555.3 15.7 %fusion.37 = f32[4304,1152]{1,0:T(8,128)} fusion(bf16[384,1152]{1,0:T(8,128)(2,1)S(1)} %bitcast.215, f32[384,4304]{0,1:T(8,128)} %get-tuple-element.275), kind=kOutput, calls=%fused_computation.107 | convolution fusion | flops 3822778368 | bytes 27328512 | tf_op jit(solution)/shard_map/dot_general | solution.py:18
  571.0 387.5 %fusion = f32[544,1152]{1,0:T(8,128)} fusion(f32[4304,1152]{1,0:T(8,128)} %fusion.37), kind=kCustom, calls=%all-reduce-scatter | all-reduce-scatter fusion | flops 5013505 | bytes 22340096
  962.8 9.9 concatenate
  976.1 45.6 %reduce-scatter.16.cloned.1.call-done = f32[144,4304]{1,0:T(8,128)} async-done(((f32[1152,4304]{1,0:T(8,128)}), f32[144,4304]{1,0:T(8,128)}) %reduce-scatter.16.cloned.1.call-update) | async-done | bytes 2479120 | tf_op jit(solution)/shard_map/reduce_scatter | solution.py:312
  1023.9 11.6 fusion.24
  1046.5 29.1 %all-reduce.20 = (f32[1152]{0:T(1024)S(1)}, f32[1152]{0:T(1024)S(1)}, f32[1152]{0:T(1024)S(1)}, f32[1152]{0:T(1024)S(1)}, f32[1152]{0:T(1024)S(1)}, /*index=5*/f...) all-reduce(f32[1152]{0:T(1024)S(1)} %get-tuple-element.175, ...), channel_id=2, replica_groups=mesh['seq'=4,'fsdp'=8] {'fsdp'}, use_global_device_ids=true, to_apply=%region_16.17.clone | all-reduce | flops 13520 | bytes 108160
  1076.2 17.0 %all-reduce.21 = (f32[144]{0:T(256)}, f32[144]{0:T(256)}, f32[144]{0:T(256)}, f32[144]{0:T(256)}, f32[144]{0:T(256)}, /*index=5*/f32[144]{0:T(256)}, f32[144]{0:T(256)}, f32[538]{0:T(1024)}, f32[144]{0:T(256)}) all-reduce(f32[144]{0:T(256)S(1)} %dynamic-slice.10, ...), channel_id=1, replica_groups=mesh['seq'=4,'fsdp'=8] {'seq'}, use_global_device_ids=true, to_apply=%region_17.18 | all-reduce | flops 1690 | bytes 13520 | tf_op jit(solution)/shard_map/psum | solution.py:317
  1096.5 91.7 %all-reduce.26.cloned.1.call-done = (f32[144,1152]{1,0:T(8,128)}, f32[144,1152]{1,0:T(8,128)}, f32[144,1152]{1,0:T(8,128)}, f32[144,1152]{1,0:T(8,128)}, f32[144,4304]{1,0:T(8,128)}, /*index=5*/f32[538,1152]{1,0:T(8,128)}) async-done(((f32[144,1152]{1,0:T(8,128)}, f32[144,1152]{1,0:T(8,128)}, f32[144,1152]{1,0:T(8,128)}, f32[144,1152]{1,0:T(8,128)}, f32[144,4304]{1,0:T(8,128)}, ...) | async-done | bytes 7612432 | tf_op jit(solution)/shard_map/psum | solution.py:317
  (314 shorter events, 174.7 us)
Async XLA Ops:
  7.3 7.2 copy-start.51
  7.3 7.5 copy-start.52
  7.3 7.7 copy-start.53
  7.3 7.9 copy-start.43
  7.3 41.6 %copy-start = (bf16[3,128,1152]{2,1,0:T(8,128)(2,1)S(1)}, bf16[3,128,1152]{2,1,0:T(8,128)(2,1)}, u32[]{:S(2)}) copy-start(bf16[3,128,1152]{2,1,0:T(8,128)(2,1)} %param.22) | copy-start | bytes 2654212
  7.3 43.8 %all-gather.8.cloned.1.call-start = ((), (), s32[]{:S(2)}) async-start(), calls=%async_computation.13 | async-start | bytes 2985984 | tf_op jit(solution)/shard_map/all_gather | solution.py:149
  8.0 74.3 %all-gather.12.cloned.1.call-start = ((), (), s32[]{:S(2)}) async-start(), calls=%async_computation.15 | async-start | bytes 2985984 | tf_op jit(solution)/shard_map/all_gather | solution.py:148
  8.8 108.4 %all-gather.10.cloned.1.call-start = ((), (), s32[]{:S(2)}) async-start(), calls=%async_computation.14 | async-start | bytes 2985984 | tf_op jit(solution)/shard_map/all_gather | solution.py:147
  9.5 185.3 %all-gather.14.cloned.1.call-start = ((), (), s32[]{:S(2)}) async-start(), calls=%async_computation.16 | async-start | bytes 2985984 | tf_op jit(solution)/shard_map/all_gather | solution.py:152
  10.1 237.9 %all-gather.18.cloned.1.call-start = ((), (), s32[]{:S(2)}) async-start(), calls=%async_computation.23 | async-start | bytes 11280384 | tf_op jit(solution)/shard_map/all_gather | solution.py:158
  10.7 332.8 %all-gather.16.cloned.1.call-start = ((), (), s32[]{:S(2)}) async-start(), calls=%async_computation.17 | async-start | bytes 11280384 | tf_op jit(solution)/shard_map/all_gather | solution.py:156
  51.1 31.3 %copy-start.17 = (bf16[384,1152]{1,0:T(8,128)(2,1)}, bf16[384,1152]{1,0:T(8,128)(2,1)S(1)}, u32[]{:S(2)}) copy-start(bf16[384,1152]{1,0:T(8,128)(2,1)S(1)} %add_convert_fusion.2) | copy-start | bytes 2654212
  56.6 33.1 %all-to-all-start = ((bf16[3,128,1152]{1,0,2:T(4,128)(2,1)}), bf16[3,128,1152]{1,0,2:T(4,128)(2,1)S(1)}, u32[]{:S(2)}, u32[]{:S(2)}) async-start(bf16[3,128,1152]{1,0,2:T(4,128)(2,1)} %copy.63), calls=%async_computation | async-start | bytes 2359296 | tf_op jit(solution)/shard_map/all_to_all | solution.py:195
  89.7 35.1 %all-to-all-start.2 = ((bf16[3,128,1152]{1,0,2:T(4,128)(2,1)}), bf16[3,128,1152]{1,0,2:T(4,128)(2,1)S(1)}, u32[]{:S(2)}, u32[]{:S(2)}) async-start(bf16[3,128,1152]{1,0,2:T(4,128)(2,1)} %copy.69), calls=%async_computation.2 | async-start | bytes 2359296 | tf_op jit(solution)/shard_map/all_to_all | solution.py:192
  121.5 7.8 copy-start.38
  124.8 20.2 %all-to-all-start.1 = ((bf16[3,128,1152]{1,0,2:T(4,128)(2,1)}), bf16[3,128,1152]{1,0,2:T(4,128)(2,1)}, u32[]{:S(2)}, u32[]{:S(2)}) async-start(bf16[3,128,1152]{1,0,2:T(4,128)(2,1)} %copy.66), calls=%async_computation.1 | async-start | bytes 2359296 | tf_op jit(solution)/shard_map/all_to_all | solution.py:189
  165.0 23.4 %all-to-all-start.3 = ((bf16[3,512,288]{2,0,1:T(4,128)(2,1)}), bf16[3,512,288]{2,0,1:T(4,128)(2,1)}, u32[]{:S(2)}, u32[]{:S(2)}) async-start(bf16[3,512,288]{2,0,1:T(4,128)(2,1)} %copy.72), calls=%async_computation.3 | async-start | bytes 3145728 | tf_op jit(solution)/shard_map/all_to_all | solution.py:201
  169.3 806.7 %reduce-scatter.14.cloned.1.call-start = ((), (), s32[]{:S(2)}) async-start(), calls=%async_computation.21 | async-start | bytes 5971968 | tf_op jit(solution)/shard_map/reduce_scatter | solution.py:308
  343.5 20.9 %copy-start.2 = (f32[384,1152]{1,0:T(8,128)S(1)}, f32[384,1152]{1,0:T(8,128)}, u32[]{:S(2)}) copy-start(f32[384,1152]{1,0:T(8,128)} %copy-done.1) | copy-start | bytes 5308420
  343.5 20.9 %copy-start.26 = (f32[384]{0:T(512)S(1)}, f32[384]{0:T(512)}, u32[]{:S(2)}) copy-start(f32[384]{0:T(512)} %add_rsqrt_fusion) | copy-start | bytes 4612
  364.4 10.7 copy-start.14
  364.4 10.7 copy-start.6
  441.6 7.0 copy-start.37
  445.0 22.2 %all-to-all-start.5 = ((bf16[3,512,288]{2,0,1:T(4,128)(2,1)}), bf16[3,512,288]{2,0,1:T(4,128)(2,1)S(1)}, u32[]{:S(2)}, u32[]{:S(2)}) async-start(bf16[3,512,288]{2,0,1:T(4,128)(2,1)} %copy.77), calls=%async_computation.5 | async-start | bytes 3145728 | tf_op jit(solution)/shard_map/all_to_all | solution.py:274
  448.5 527.5 %reduce-scatter.8.cloned.1.call-start = ((), (), s32[]{:S(2)}) async-start(), calls=%async_computation.18 | async-start | bytes 5971968 | tf_op jit(solution)/shard_map/reduce_scatter | solution.py:303
  476.1 500.0 %reduce-scatter.10.cloned.1.call-start = ((), (), s32[]{:S(2)}) async-start(), calls=%async_computation.19 | async-start | bytes 5971968 | tf_op jit(solution)/shard_map/reduce_scatter | solution.py:304
  508.9 467.2 %reduce-scatter.12.cloned.1.call-start = ((), (), s32[]{:S(2)}) async-start(), calls=%async_computation.20 | async-start | bytes 5971968 | tf_op jit(solution)/shard_map/reduce_scatter | solution.py:305
  541.0 480.7 %reduce-scatter.16.cloned.1.call-start = ((), (), s32[]{:S(2)}) async-start(), calls=%async_computation.22 | async-start | bytes 22560768 | tf_op jit(solution)/shard_map/reduce_scatter | solution.py:312
  554.1 634.1 %all-reduce.26.cloned.1.call-start = ((), (), s32[]{:S(2)}) async-start(), calls=%async_computation.24 | async-start | bytes 15335424 | tf_op jit(solution)/shard_map/psum | solution.py:317
  960.1 2.7 collective-permute-start
  1023.9 13.8 %copy-start.10 = (bf16[384,1152]{1,0:T(8,128)(2,1)S(1)}, bf16[384,1152]{1,0:T(8,128)(2,1)}, u32[]{:S(2)}) copy-start(bf16[384,1152]{1,0:T(8,128)(2,1)} %copy-done.9) | copy-start | bytes 2654212
  1043.5 49.7 %copy-start.5 = (f32[384,1152]{1,0:T(8,128)S(1)}, f32[384,1152]{1,0:T(8,128)}, u32[]{:S(2)}) copy-start(f32[384,1152]{1,0:T(8,128)} %copy-done.4) | copy-start | bytes 5308420
  (40 other events, 127.0 us)
Sparse Core Ops, SparseCore 0:
  9.8 37.7 all-gather.7
  49.1 33.1 all-gather.11
  84.0 33.0 all-gather.9
  118.6 33.0 all-gather.13
  153.3 94.6 all-gather.17
  249.5 93.9 all-gather.15
  381.8 58.8 reduce-scatter.13
  476.2 57.8 reduce-scatter.7
  536.4 74.3 reduce-scatter.9
  612.9 111.5 reduce-scatter.11
  726.9 294.8 reduce-scatter.15
  1026.6 161.5 all-reduce.25
where the time goes:
time: 1210 us
  blocking collectives  529 us (44%)
  waiting for transfers between devices  355 us (29%)
  matrix products  148 us (12%)
  local copies, waits for them, and re-layouts  111 us (9%)
  starting transfers between devices  22.1 us (2%)
  other arithmetic  21 us (2%)
  between operations  18.5 us (2%)
    unnamed x3, blocking collectives  450 us
    psum x1, waiting for transfers between devices, shards(): lax.psum((shard_grads[0], shard_grads[1], shard_grads[2], shard_grads[3],...  91.7 us
    all_gather x1, waiting for transfers between devices, shards(): lax.all_gather(inner_weight, 'fsdp', axis=0, tiled=True)  72.6 us
    dot_general x6, matrix products, product(): return jnp.dot(left, right, preferred_element_type=jnp.float32)  48 us
    unnamed x146, local copies, waits for them, and re-layouts  47.9 us
    all_gather x1, waiting for transfers between devices, shards(): lax.all_gather(outer_weight, 'fsdp', axis=0, tiled=True)  47.5 us
    dot_general x6, matrix products, product_rows(): lax.dot_general(left, right, (((0,), (0,)), ((), ())), preferred_element_...  45.7 us
    reduce_scatter x1, waiting for transfers between devices, shards(): lax.psum_scatter(mlp_terms[2], 'fsdp', scatter_dimension=0, tiled=True)  45.6 us
  transfers between devices with their start and end apart: 18, of which 10 were waited for; matrix products, arithmetic and copies ran while one was open for 51% of the time, Pallas kernels for 0%

commit v1 on v0

v1 whole, which is shorter than its diff:
```python
import functools

import jax
import jax.numpy as jnp
from jax import lax
from jax.experimental import pallas as pl
from jax.experimental.pallas import tpu as pltpu
from jax.sharding import PartitionSpec as P

HD = 72
EPSILON = 1e-06
MASKED = -1e30
MESH = pl.DeviceIdType.MESH
VMEM_LIMIT = 64_000_000


def flip(index, bit):
    on = lax.rem(lax.div(index, 1 << bit), 2)
    return index + (1 - 2 * on) * (1 << bit)


def flip_mask(index, mask):
    bit = 0
    while mask >> bit:
        if (mask >> bit) & 1:
            index = flip(index, bit)
        bit += 1
    return index


def halving(bits, parts):
    plan = []
    for j in range(parts):
        held, steps, slot = [0], [], 0
        for k in range(bits):
            bit = (j + k) % bits
            steps.append((bit, tuple(held), slot))
            slot += len(held)
            held = held + [m ^ (1 << bit) for m in held]
        plan.append(steps)
    return plan


def copy_to(src, dst, send, recv, seq, fsdp):
    return pltpu.make_async_remote_copy(
        src_ref=src,
        dst_ref=dst,
        send_sem=send,
        recv_sem=recv,
        device_id={"seq": seq, "fsdp": fsdp},
        device_id_type=MESH,
    )


def greet(s, f, n_seq, n_fsdp):
    core, zed = lax.rem(f, 2), lax.div(f, 2)
    n_z = n_fsdp // 2
    barrier = pltpu.get_barrier_semaphore()
    peers = [(s, f + 1 - 2 * core)]
    peers += [(s, lax.rem(zed + d, n_z) * 2 + core) for d in range(1, n_z)]
    bit = 0
    while (1 << bit) < n_seq:
        peers.append((flip(s, bit), f))
        bit += 1
    for seq, fsdp in peers:
        pl.semaphore_signal(
            barrier, inc=1, device_id={"seq": seq, "fsdp": fsdp}, device_id_type=MESH
        )
    pl.semaphore_wait(barrier, len(peers))


def gather_kernel(n_seq, n_fsdp, packs, parts, *refs):
    own = refs[:packs]
    vec = refs[packs]
    full = refs[packs + 1 : 2 * packs + 1]
    vec_full = refs[2 * packs + 1]
    z_send, z_recv, p_send, p_recv, c_send, c_recv, v_send, v_recv, local = refs[2 * packs + 2 :]
    s, f = lax.axis_index("seq"), lax.axis_index("fsdp")
    core, zed = lax.rem(f, 2), lax.div(f, 2)
    n_z = n_fsdp // 2
    bits = n_seq.bit_length() - 1
    plan = halving(bits, parts)
    other = f + 1 - 2 * core
    from_f = [lax.rem(zed - d + n_z, n_z) * 2 + core for d in range(n_z)]
    to_f = [lax.rem(zed + d, n_z) * 2 + core for d in range(n_z)]
    greet(s, f, n_seq, n_fsdp)

    def z_copy(p, d):
        return copy_to(
            own[p].at[s], full[p].at[s, f], z_send.at[p, d], z_recv.at[p, d], s, to_f[d]
        )

    def z_arrival(p, d):
        return copy_to(
            own[p].at[s], full[p].at[s, from_f[d]], z_send.at[p, d], z_recv.at[p, d], s, to_f[d]
        )

    def plane_copies(p, d, k, arriving):
        out = []
        for j in range(parts):
            bit, held, slot = plan[j][k]
            for i, mask in enumerate(held):
                place = full[p].at[flip_mask(s, mask), from_f[d], j]
                arrive = full[p].at[flip_mask(s, mask ^ (1 << bit)), from_f[d], j]
                sems = p_send.at[p, d, j, slot + i], p_recv.at[p, d, j, slot + i]
                target = arrive if arriving else place
                out.append(copy_to(place, target, *sems, flip(s, bit), f))
        return out

    def core_copy(p, d):
        return copy_to(
            full[p].at[:, from_f[d]],
            full[p].at[:, from_f[d]],
            c_send.at[p, d],
            c_recv.at[p, d],
            s,
            other,
        )

    def core_first(p):
        return copy_to(own[p], full[p].at[:, f], c_send.at[p, 0], c_recv.at[p, 0], s, other)

    def core_arrival(p, d):
        place = full[p].at[:, from_f[d] + 1 - 2 * core]
        return copy_to(place, place, c_send.at[p, d], c_recv.at[p, d], s, other)

    sent = []

    def start(copy):
        copy.start()
        sent.append(copy)

    vec_targets = [to_f[d] for d in range(1, n_z)] + [other]
    for i, target in enumerate(vec_targets):
        start(copy_to(vec, vec_full.at[f], v_send.at[i], v_recv.at[i], s, target))
    for p in range(packs):
        for d in range(1, n_z):
            start(z_copy(p, d))
    keep = [pltpu.make_async_copy(own[p], full[p].at[:, f], local.at[p]) for p in range(packs)]
    keep.append(pltpu.make_async_copy(vec, vec_full.at[f], local.at[packs]))
    for copy in keep:
        copy.start()
    for p in range(packs):
        start(core_first(p))
    for d in range(1, n_z):
        copy_to(vec, vec_full.at[from_f[d]], v_send.at[d - 1], v_recv.at[d - 1], s, to_f[d]).wait_recv()
        start(
            copy_to(
                vec_full.at[from_f[d]],
                vec_full.at[from_f[d]],
                v_send.at[n_z - 1 + d],
                v_recv.at[n_z - 1 + d],
                s,
                other,
            )
        )

    def finish(p, d):
        for arrival in plane_copies(p, d, bits - 1, True):
            arrival.wait_recv()
        start(core_copy(p, d))

    for p in range(packs + 1):
        for d in range(1, n_z):
            if p < packs:
                z_arrival(p, d).wait_recv()
                for copy in plane_copies(p, d, 0, False):
                    start(copy)
            if p > 0:
                finish(p - 1, d)
        if p < packs:
            for k in range(1, bits):
                for d in range(1, n_z):
                    for arrival in plane_copies(p, d, k - 1, True):
                        arrival.wait_recv()
                    for copy in plane_copies(p, d, k, False):
                        start(copy)
    for copy in keep:
        copy.wait()
    for p in range(packs):
        for d in range(n_z):
            core_arrival(p, d).wait_recv()
    for d in range(n_z):
        place = vec_full.at[from_f[d] + 1 - 2 * core]
        sem = n_z - 1 + d
        copy_to(place, place, v_send.at[sem], v_recv.at[sem], s, other).wait_recv()
    for copy in sent:
        copy.wait_send()


def gather_all(n_seq, n_fsdp, blocks, vec):
    packs, parts = len(blocks), blocks[0].shape[1]
    n_z = n_fsdp // 2
    dma = pltpu.SemaphoreType.DMA
    out = [
        jax.ShapeDtypeStruct((b.shape[0], n_fsdp) + b.shape[1:], b.dtype) for b in blocks
    ] + [jax.ShapeDtypeStruct((n_fsdp,) + vec.shape, vec.dtype)]
    return pl.pallas_call(
        functools.partial(gather_kernel, n_seq, n_fsdp, packs, parts),
        out_shape=out,
        in_specs=[pl.BlockSpec(memory_space=pltpu.VMEM)] * (packs + 1),
        out_specs=[pl.BlockSpec(memory_space=pl.ANY)] * (packs + 1),
        scratch_shapes=[
            dma((packs, n_z)),
            dma((packs, n_z)),
            dma((packs, n_z, parts, n_seq - 1)),
            dma((packs, n_z, parts, n_seq - 1)),
            dma((packs, n_z)),
            dma((packs, n_z)),
            dma((2 * n_z - 1,)),
            dma((2 * n_z - 1,)),
            dma((packs + 1,)),
        ],
        compiler_params=pltpu.CompilerParams(
            collective_id=0, has_side_effects=True, vmem_limit_bytes=VMEM_LIMIT
        ),
        name="gather_weights",
    )(*blocks, vec)


def add_into(target, term, rows):
    target[...] = (target[...].astype(jnp.float32) + term[...].astype(jnp.float32)).astype(
        target.dtype
    )


def reduce_kernel(n_seq, n_fsdp, packs, parts, *refs):
    share = n_seq // 4
    n_grads = 4 * packs
    grads = refs[:n_grads]
    vec = refs[n_grads]
    out = refs[n_grads + 1 : n_grads + 1 + packs]
    vec_out = refs[n_grads + 1 + packs]
    (
        held,
        part_in,
        plane_in,
        z_in,
        total,
        v_core,
        v_plane,
        v_z,
        v_work,
        l_sem,
        c_send,
        c_recv,
        p_send,
        p_recv,
        z_send,
        z_recv,
        g_send,
        g_recv,
        v_send,
        v_recv,
        o_sem,
    ) = refs[n_grads + 2 + packs :]
    s, f = lax.axis_index("seq"), lax.axis_index("fsdp")
    core, zed = lax.rem(f, 2), lax.div(f, 2)
    n_z = n_fsdp // 2
    bits = n_seq.bit_length() - 1
    plan = halving(bits, parts)
    other = f + 1 - 2 * core
    to_f = [lax.rem(zed + d, n_z) * 2 + core for d in range(n_z)]
    greet(s, f, n_seq, n_fsdp)
    sent = []

    def start(copy):
        copy.start()
        sent.append(copy)

    def target_z(t):
        return lax.rem(zed + t + 1, n_z)

    def load(p, t):
        out = []
        for q in range(n_seq):
            src = grads[4 * p + q // share]
            out.append(
                pltpu.make_async_copy(
                    src.at[2 * target_z(t) + core, q % share],
                    held.at[p, t, q],
                    l_sem.at[p, t, q],
                )
            )
        return out

    def to_partner(p, t):
        out = []
        for q in range(n_seq):
            src = grads[4 * p + q // share]
            out.append(
                copy_to(
                    src.at[2 * target_z(t) + 1 - core, q % share],
                    part_in.at[p, t, q],
                    c_send.at[p, t, q],
                    c_recv.at[p, t, q],
                    s,
                    other,
                )
            )
        return out

    def plane(p, t, k):
        out = []
        for j in range(parts):
            bit, masks, slot = plan[j][k]
            for i, mask in enumerate(masks):
                out.append(
                    (
                        copy_to(
                            held.at[p, t, flip_mask(s, mask ^ (1 << bit)), j],
                            plane_in.at[p, t, j, slot + i],
                            p_send.at[p, t, j, slot + i],
                            p_recv.at[p, t, j, slot + i],
                            flip(s, bit),
                            f,
                        ),
                        held.at[p, t, flip_mask(s, mask), j],
                        plane_in.at[p, t, j, slot + i],
                    )
                )
        return out

    def z_copy(p, t):
        return copy_to(
            held.at[p, t, s],
            z_in.at[p, t],
            z_send.at[p, t],
            z_recv.at[p, t],
            s,
            2 * target_z(t) + core,
        )

    def spread(p, k, arriving):
        out = []
        for j in range(parts):
            bit, masks, slot = plan[j][k]
            for i, mask in enumerate(masks):
                place = total.at[p, flip_mask(s, mask), j]
                arrive = total.at[p, flip_mask(s, mask ^ (1 << bit)), j]
                sems = g_send.at[p, j, slot + i], g_recv.at[p, j, slot + i]
                target = arrive if arriving else place
                out.append(copy_to(place, target, *sems, flip(s, bit), f))
        return out

    chunks = [(p, t) for p in range(packs) for t in range(n_z)]
    v_part = copy_to(
        vec.at[:, 1 - core], v_core, v_send.at[0], v_recv.at[0], s, other
    )
    start(v_part)
    for p, t in chunks:
        for copy in to_partner(p, t):
            start(copy)
        for copy in load(p, t):
            copy.start()

    def stage_core(p, t):
        for copy, arrival in zip(load(p, t), to_partner(p, t)):
            copy.wait()
            arrival.wait_recv()
        for q in range(n_seq):
            add_into(held.at[p, t, q], part_in.at[p, t, q], None)
        for copy, _, _ in plane(p, t, bits - 1):
            start(copy)

    def stage_plane(p, t, k):
        for copy, mine, came in plane(p, t, k):
            copy.wait_recv()
            add_into(mine, came, None)
        if k > 0:
            for copy, _, _ in plane(p, t, k - 1):
                start(copy)
        elif t < n_z - 1:
            start(z_copy(p, t))

    def stage_total(p):
        for t in range(n_z - 1):
            z_copy(p, t).wait_recv()
        for j in range(parts):
            value = held[p, n_z - 1, s, j].astype(jnp.float32)
            for t in range(n_z - 1):
                value = value + z_in[p, t, j].astype(jnp.float32)
            total[p, s, j] = value.astype(total.dtype)
        for copy in spread(p, 0, False):
            start(copy)

    def stage_spread(p, k):
        for arrival in spread(p, k - 1, True):
            arrival.wait_recv()
        if k < bits:
            for copy in spread(p, k, False):
                start(copy)
        else:
            pltpu.make_async_copy(total.at[p], out[p], o_sem.at[p]).start()

    def vec_stage(i):
        if i == 0:
            v_part.wait_recv()
            v_work[0] = vec[:, core] + v_core[...]
        if 0 < i <= bits:
            copy_to(
                v_work.at[i - 1], v_plane.at[i - 1], v_send.at[i], v_recv.at[i], flip(s, i - 1), f
            ).wait_recv()
            v_work[i] = v_work[i - 1] + v_plane[i - 1]
        if i < bits:
            start(
                copy_to(
                    v_work.at[i], v_plane.at[i], v_send.at[i + 1], v_recv.at[i + 1], flip(s, i), f
                )
            )
        if i == bits:
            for d in range(1, n_z):
                start(
                    copy_to(
                        v_work.at[bits, lax.rem(zed + d, n_z)],
                        v_z.at[d - 1],
                        v_send.at[bits + d],
                        v_recv.at[bits + d],
                        s,
                        to_f[d],
                    )
                )
        if i == bits + 1:
            value = v_work[bits, zed]
            for d in range(1, n_z):
                copy_to(
                    v_work.at[bits, zed],
                    v_z.at[d - 1],
                    v_send.at[bits + d],
                    v_recv.at[bits + d],
                    s,
                    to_f[d],
                ).wait_recv()
                value = value + v_z[d - 1]
            vec_out[...] = value

    n = len(chunks)
    events = []
    for i in range(n):
        events.append((i, 0, functools.partial(stage_core, *chunks[i])))
        for e, k in enumerate(range(bits - 1, -1, -1)):
            events.append((i + 1 + e, 1 + e, functools.partial(stage_plane, *chunks[i], k)))
    for p in range(packs):
        last = (p + 1) * n_z - 1 + bits
        events.append((last + 2, 20, functools.partial(stage_total, p)))
        for k in range(1, bits + 1):
            events.append((last + 2 + k, 20 + k, functools.partial(stage_spread, p, k)))
    for i in range(bits + 2):
        events.append((i + 1, 40, functools.partial(vec_stage, i)))
    for _, _, run in sorted(events, key=lambda e: e[:2]):
        run()
    for p in range(packs):
        pltpu.make_async_copy(total.at[p], out[p], o_sem.at[p]).wait()
    for copy in sent:
        copy.wait_send()


def reduce_all(n_seq, n_fsdp, parts, grads, vec, collective_id):
    packs = len(grads) // 4
    n_z = n_fsdp // 2
    bits = n_seq.bit_length() - 1
    piece = grads[0].shape[2:]
    low, dma, vmem = grads[0].dtype, pltpu.SemaphoreType.DMA, pltpu.VMEM
    vshape = vec.shape[2:]
    return pl.pallas_call(
        functools.partial(reduce_kernel, n_seq, n_fsdp, packs, parts),
        out_shape=[jax.ShapeDtypeStruct((n_seq,) + piece, low) for _ in range(packs)]
        + [jax.ShapeDtypeStruct(vshape, vec.dtype)],
        in_specs=[pl.BlockSpec(memory_space=pl.ANY)] * len(grads)
        + [pl.BlockSpec(memory_space=pltpu.VMEM)],
        out_specs=[pl.BlockSpec(memory_space=pl.ANY)] * packs
        + [pl.BlockSpec(memory_space=pltpu.VMEM)],
        scratch_shapes=[
            vmem((packs, n_z, n_seq) + piece, low),
            vmem((packs, n_z, n_seq) + piece, low),
            vmem((packs, n_z, parts, n_seq - 1) + piece[1:], low),
            vmem((packs, n_z - 1) + piece, low),
            vmem((packs, n_seq) + piece, low),
            vmem((n_z,) + vshape, vec.dtype),
            vmem((bits, n_z) + vshape, vec.dtype),
            vmem((n_z - 1,) + vshape, vec.dtype),
            vmem((bits + 1, n_z) + vshape, vec.dtype),
            dma((packs, n_z, n_seq)),
            dma((packs, n_z, n_seq)),
            dma((packs, n_z, n_seq)),
            dma((packs, n_z, parts, n_seq - 1)),
            dma((packs, n_z, parts, n_seq - 1)),
            dma((packs, n_z)),
            dma((packs, n_z)),
            dma((packs, parts, n_seq - 1)),
            dma((packs, parts, n_seq - 1)),
            dma((bits + n_z,)),
            dma((bits + n_z,)),
            dma((packs,)),
        ],
        compiler_params=pltpu.CompilerParams(
            collective_id=collective_id, has_side_effects=True, vmem_limit_bytes=VMEM_LIMIT
        ),
        name="reduce_grads",
    )(*grads, vec)


def product(left, right):
    return jnp.dot(left, right, preferred_element_type=jnp.float32)


def product_rows(left, right):
    return lax.dot_general(
        left, right, (((0,), (0,)), ((), ())), preferred_element_type=jnp.float32
    )


def product_back(left, right):
    return lax.dot_general(
        left, right, (((1,), (1,)), ((), ())), preferred_element_type=jnp.float32
    )


def gelu_tanh(values):
    return jax.nn.gelu(values, approximate=True)


def normalize(values):
    center = values - jnp.mean(values, axis=-1, keepdims=True)
    factor = lax.rsqrt(jnp.mean(center * center, axis=-1, keepdims=True) + EPSILON)
    return (center * factor, factor)


def norm_back(grad_normed, normed, factor):
    first = jnp.mean(grad_normed, axis=-1, keepdims=True)
    second = jnp.mean(grad_normed * normed, axis=-1, keepdims=True)
    return factor * (grad_normed - first - normed * second)


def wide(values):
    return values.astype(jnp.float32)


def forward_image(items):
    query, keys, values, valid = items
    length, local = query.shape
    heads = local // HD
    scale = HD ** (-0.5)
    query_three = query.reshape(length, heads, HD)
    key_three = keys.reshape(length, heads, HD)
    value_three = values.reshape(length, heads, HD)
    scores = (
        jnp.einsum("qhd,khd->hqk", query_three, key_three, preferred_element_type=jnp.float32)
        * scale
    )
    scores = jnp.where(valid[None, None, :], scores, MASKED)
    highest = jnp.max(scores, axis=-1, keepdims=True)
    logsum = highest + jnp.log(jnp.sum(jnp.exp(scores - highest), axis=-1, keepdims=True))
    attention = jnp.exp(scores - logsum).astype(jnp.bfloat16)
    attended = jnp.einsum(
        "hqk,khd->qhd", attention, value_three, preferred_element_type=jnp.float32
    )
    return (attended.astype(jnp.bfloat16).reshape(length, local), logsum[..., 0])


def backward_image(items):
    query, keys, values, attended, grad_out, logsum, valid = items
    length, local = query.shape
    heads = local // HD
    scale = HD ** (-0.5)
    query, keys, values, attended, grad_out = (
        item.reshape(length, heads, HD) for item in (query, keys, values, attended, grad_out)
    )
    scores = jnp.einsum("qhd,khd->hqk", query, keys, preferred_element_type=jnp.float32) * scale
    scores = jnp.where(valid[None, None, :], scores, MASKED)
    chance = jnp.exp(scores - logsum[:, :, None])
    chance_low = chance.astype(jnp.bfloat16)
    grad_values = jnp.einsum(
        "hqk,qhd->khd", chance_low, grad_out, preferred_element_type=jnp.float32
    )
    grad_chance = jnp.einsum("qhd,khd->hqk", grad_out, values, preferred_element_type=jnp.float32)
    delta = jnp.sum(wide(grad_out) * wide(attended), axis=-1).T
    grad_scores = (chance * (grad_chance - delta[:, :, None]) * scale).astype(jnp.bfloat16)
    grad_query = jnp.einsum("hqk,khd->qhd", grad_scores, keys, preferred_element_type=jnp.float32)
    grad_keys = jnp.einsum("hqk,qhd->khd", grad_scores, query, preferred_element_type=jnp.float32)
    return tuple(
        item.astype(jnp.bfloat16).reshape(length, local)
        for item in (grad_query, grad_keys, grad_values)
    )


def to_heads(tokens):
    return lax.all_to_all(tokens, "seq", split_axis=2, concat_axis=1, tiled=True)


def to_tokens(heads):
    return lax.all_to_all(heads, "seq", split_axis=1, concat_axis=2, tiled=True)


def shards(
    n_seq,
    n_fsdp,
    images,
    key_mask,
    attn_gain,
    attn_shift,
    query_weight,
    key_weight,
    value_weight,
    query_bias,
    value_bias,
    out_weight,
    out_bias,
    mlp_gain,
    mlp_shift,
    inner_weight,
    inner_bias,
    outer_weight,
    outer_bias,
    cotangent,
):
    count, block_len, width = images.shape
    rows = count * block_len
    low = images.dtype
    depth = query_weight.shape[0]
    ff_own = outer_weight.shape[0]
    slack = 4 * depth - ff_own
    bits = n_seq.bit_length() - 1
    piece = 4 * depth // n_seq
    parts = bits if piece % (8 * bits) == 0 else 1
    shape = (parts, piece // parts, width)

    inner_cols = jnp.pad(
        inner_weight.reshape(depth, n_fsdp, ff_own), ((0, 0), (0, 0), (0, slack))
    ).reshape(depth, n_fsdp, 4, depth)
    packed = (
        jnp.stack((query_weight, key_weight, value_weight, out_weight)),
        inner_cols.transpose(2, 0, 1, 3).reshape(4, depth, width),
        jnp.pad(outer_weight, ((0, slack), (0, 0))),
    )
    small = jnp.concatenate(
        (
            attn_gain,
            attn_shift,
            query_bias,
            value_bias,
            out_bias,
            mlp_gain,
            mlp_shift,
            outer_bias,
            inner_bias,
        )
    )
    vec_rows = -(-small.shape[0] // 2048) * 16
    vec = jnp.pad(small, (0, vec_rows * 128 - small.shape[0])).reshape(vec_rows, 128)
    *full, vec_full = gather_all(
        n_seq, n_fsdp, [item.reshape((n_seq,) + shape) for item in packed], vec
    )

    def square(item):
        return (
            item.reshape(4, n_seq // 4, n_fsdp, piece, width)
            .swapaxes(1, 2)
            .reshape(4, width, width)
        )

    w_attn, w_inner, w_outer = (square(item) for item in full)
    w_query, w_key, w_value, w_out = (w_attn[i] for i in range(4))
    flat_vec = wide(vec_full.reshape(n_fsdp, vec_rows * 128))
    gain_attn, shift_attn, b_query, b_value, b_out, gain_mlp, shift_mlp, b_outer = (
        flat_vec[:, i * depth : (i + 1) * depth].reshape(width) for i in range(8)
    )
    b_inner = (
        jnp.pad(flat_vec[:, 8 * depth : 8 * depth + ff_own], ((0, 0), (0, slack)))
        .reshape(n_fsdp, 4, depth)
        .transpose(1, 0, 2)
        .reshape(4, width)
    )

    flat = wide(images.reshape(rows, width))
    normed_one, factor_one = normalize(flat)
    hidden_one = (normed_one * gain_attn + shift_attn).astype(low)
    query = (product(hidden_one, w_query) + b_query).astype(low)
    keys = product(hidden_one, w_key).astype(low)
    values = (product(hidden_one, w_value) + b_value).astype(low)
    tokens = (count, block_len, width)
    query_heads, key_heads, value_heads = (
        to_heads(item.reshape(tokens)) for item in (query, keys, values)
    )
    valid = key_mask > 0
    attended, logsum = lax.map(forward_image, (query_heads, key_heads, value_heads, valid))
    attended_flat = to_tokens(attended).reshape(rows, width)
    second = flat + product(attended_flat, w_out) + b_out
    normed_two, factor_two = normalize(second)
    hidden_two = (normed_two * gain_mlp + shift_mlp).astype(low)
    inner = [product(hidden_two, w_inner[i]) + b_inner[i] for i in range(4)]
    active = [gelu_tanh(item).astype(low) for item in inner]
    outer = sum(product(active[i], w_outer[i]) for i in range(4))
    layer_out = second + outer + b_outer

    upstream = cotangent.reshape(rows, width)
    grad_inner = [
        jax.vjp(gelu_tanh, inner[i])[1](product_back(upstream, w_outer[i]))[0] for i in range(4)
    ]
    grad_inner_low = [item.astype(low) for item in grad_inner]
    grad_hidden_two = sum(product_back(grad_inner_low[i], w_inner[i]) for i in range(4))
    grad_second = wide(upstream) + norm_back(grad_hidden_two * gain_mlp, normed_two, factor_two)
    grad_second_low = grad_second.astype(low)

    grad_attended = product_back(grad_second_low, w_out).astype(low)
    grad_heads = to_heads(grad_attended.reshape(tokens))
    grad_query, grad_keys, grad_values = (
        to_tokens(item).reshape(rows, width)
        for item in lax.map(
            backward_image,
            (query_heads, key_heads, value_heads, attended, grad_heads, logsum, valid),
        )
    )
    grad_hidden_one = (
        product_back(grad_query, w_query)
        + product_back(grad_keys, w_key)
        + product_back(grad_values, w_value)
    )
    images_grad = grad_second + norm_back(grad_hidden_one * gain_attn, normed_one, factor_one)

    squares = [
        product_rows(hidden_one, grad_query),
        product_rows(hidden_one, grad_keys),
        product_rows(hidden_one, grad_values),
        product_rows(attended_flat, grad_second_low),
    ]
    squares += [product_rows(hidden_two, item) for item in grad_inner_low]
    squares += [product_rows(item, upstream) for item in active]
    sums = [
        jnp.sum(grad_hidden_one * normed_one, axis=0),
        jnp.sum(grad_hidden_one, axis=0),
        jnp.sum(wide(grad_query), axis=0),
        jnp.sum(wide(grad_values), axis=0),
        jnp.sum(grad_second, axis=0),
        jnp.sum(grad_hidden_two * normed_two, axis=0),
        jnp.sum(grad_hidden_two, axis=0),
        jnp.sum(wide(upstream), axis=0),
    ]
    inner_sum = (
        jnp.stack([jnp.sum(item, axis=0) for item in grad_inner])
        .reshape(4, n_fsdp, depth)
        .transpose(1, 0, 2)
        .reshape(n_fsdp, 4 * depth)[:, :ff_own]
    )
    vec_grad = jnp.concatenate([item.reshape(n_fsdp, depth) for item in sums] + [inner_sum], axis=1)
    vec_grad = jnp.pad(vec_grad, ((0, 0), (0, vec_rows * 128 - vec_grad.shape[1])))
    *reduced, vec_sum = reduce_all(
        n_seq,
        n_fsdp,
        parts,
        [item.astype(low).reshape((n_fsdp, n_seq // 4) + shape) for item in squares],
        vec_grad.reshape(n_fsdp // 2, 2, vec_rows, 128),
        1,
    )
    attn, inn, out = (wide(item).reshape(4, depth, width) for item in reduced)
    inner_grad = (
        inn.reshape(4, depth, n_fsdp, depth)
        .transpose(1, 2, 0, 3)
        .reshape(depth, n_fsdp, 4 * depth)[:, :, :ff_own]
        .reshape(inner_weight.shape)
    )
    outer_grad = out.reshape(4 * depth, width)[:ff_own]
    sums = vec_sum.reshape(vec_rows * 128)
    small_grads = [sums[i * depth : (i + 1) * depth] for i in range(8)]
    return (
        layer_out.reshape(tokens),
        images_grad.reshape(tokens),
        small_grads[0],
        small_grads[1],
        attn[0],
        attn[1],
        attn[2],
        small_grads[2],
        small_grads[3],
        attn[3],
        small_grads[4],
        small_grads[5],
        small_grads[6],
        inner_grad,
        sums[8 * depth : 8 * depth + ff_own],
        outer_grad,
        small_grads[7],
    )


def solution(mesh):
    vector, matrix, tokens = P("fsdp"), P("fsdp", None), P("fsdp", "seq", None)
    params = (
        vector,
        vector,
        matrix,
        matrix,
        matrix,
        vector,
        vector,
        matrix,
        vector,
        vector,
        vector,
        matrix,
        vector,
        matrix,
        vector,
    )
    return jax.shard_map(
        functools.partial(shards, mesh.shape["seq"], mesh.shape["fsdp"]),
        mesh=mesh,
        in_specs=(tokens, matrix) + params + (tokens,),
        out_specs=(tokens, tokens) + params,
        check_vma=False,
    )
```

time: 1210 us -> 736 us (0.61)
  blocking collectives: 529 us -> 0 us
  Pallas kernels: 0 us -> 323 us
  waiting for transfers between devices: 355 us -> 46.6 us
  local copies, waits for them, and re-layouts: 111 us -> 166 us
  matrix products: 148 us -> 129 us
  between operations: 18.5 us -> 2.01 us
    unnamed x3 -> x0, blocking collectives: 450 us -> none
    pallas_call x0 -> x2, Pallas kernels: none -> 323 us  [the longest x1 184 us: reduce_all(): pl.pallas_call(functools.partial(reduce_kernel, n_seq, n_fsdp, packs, par...]
    all_gather x6 -> x0, waiting for transfers between devices: 166 us -> none  [the longest x1 72.6 us: shards(): lax.all_gather(inner_weight, 'fsdp', axis=0, tiled=True)]
    psum x1 -> x0, waiting for transfers between devices: 91.7 us -> none  [shards(): lax.psum((shard_grads[0], shard_grads[1], shard_grads[2], shard_grads[3],...]
    all_to_all x3 -> x0, blocking collectives: 62.3 us -> none  [the longest x1 21.9 us: shards(): lax.all_to_all(grad_key_heads, 'seq', split_axis=1, concat_axis=2, tiled=...]
    reduce_scatter x5 -> x0, waiting for transfers between devices: 45.7 us -> none  [the longest x1 45.6 us: shards(): lax.psum_scatter(mlp_terms[2], 'fsdp', scatter_dimension=0, tiled=True)]
    unnamed x146 -> x155, local copies, waits for them, and re-layouts: 47.9 us -> 9.89 us
    slice x0 -> x8, local copies, waits for them, and re-layouts: none -> 31.4 us  [the longest x2 16.4 us: shards(): inner = [product(hidden_two, w_inner[i]) + b_inner[i] for i in range(4)]]
  transfers between devices with their start and end apart: 18 -> 8, of which waited for: 10 -> 6; matrix products, arithmetic and copies ran while one was open for 51% -> 15% of each run, Pallas kernels for 0% -> 0%
where the time goes in v1:
time: 736 us; the launch traced here: 724 us
  Pallas kernels  323 us (44%)
  local copies, waits for them, and re-layouts  166 us (23%)
  matrix products  129 us (18%)
  waiting for transfers between devices  46.6 us (6%)
  starting transfers between devices  32 us (4%)
  other arithmetic  24.9 us (3%)
    pallas_call x1, Pallas kernels, reduce_all(): pl.pallas_call(functools.partial(reduce_kernel, n_seq, n_fsdp, packs, par...  184 us
    pallas_call x1, Pallas kernels, gather_all(): pl.pallas_call(functools.partial(gather_kernel, n_seq, n_fsdp, packs, par...  140 us
    dot_general x12, matrix products, product_rows(): lax.dot_general(left, right, (((0,), (0,)), ((), ())), preferred_element_...  43.4 us
    dot_general x12, matrix products, product(): return jnp.dot(left, right, preferred_element_type=jnp.float32)  36.6 us
    all_to_all x4, waiting for transfers between devices, to_heads(): lax.all_to_all(tokens, 'seq', split_axis=2, concat_axis=1, tiled=True)  28.8 us
    dot_general x12, matrix products, product_back(): lax.dot_general(left, right, (((1,), (1,)), ((), ())), preferred_element_...  28 us
    all_to_all x4, waiting for transfers between devices, to_tokens(): return lax.all_to_all(heads, 'seq', split_axis=1, concat_axis=2, tiled=True)  17.8 us
    slice x2, local copies, waits for them, and re-layouts, shards(): inner = [product(hidden_two, w_inner[i]) + b_inner[i] for i in range(4)]  16.4 us
  transfers between devices with their start and end apart: 8, of which 6 were waited for; matrix products, arithmetic and copies ran while one was open for 15% of the time, Pallas kernels for 0%

profile of v1, /device:TPU:0, one launch (start us, length us, event | category | flops | bytes accessed | tf_op | source)
XLA Modules:
  0.0 723.8 jit_solution(697292903516214856)
XLA Ops:
  16.4 139.8 %gather_weights.1 = (bf16[4,8,2,72,1152]{4,3,2,1,0:T(8,128)(2,1)}, bf16[4,8,2,72,1152]{4,3,2,1,0:T(8,128)(2,1)}, bf16[4,8,2,72,1152]{4,3,2,1,0:T(8,128)(2,1)}, bf16[8,16,128]{2,1,0:T(8,128)(2,1)}) custom-call(bf16[4,2,72,1152]{3,2,1,0:T(8,128)(2,1)} %pad_maximum_fusion.refs_0_, bf16[4,2,72,1152]{3,2,1,0:T(8,128)(2,1)} %reshape_reshape.11.refs_1_, ...), custom_call_target="tpu_custom_call" | custom-call | tf_op jit(solution)/shard_map/gather_weights/pallas_call | solution.py:198
  160.4 7.3 %fusion.63 = (bf16[1,8,2,72,1152]{4,3,2,1,0:T(8,128)(2,1)}, bf16[1,8,2,72,1152]{4,3,2,1,0:T(8,128)(2,1)}, bf16[1,8,2,72,1152]{4,3,2,1,0:T(8,128)(2,1)}, bf16[1,8,2,72,1152]{4,3,2,1,0:T(8,128)(2,1)S(1)}) fusion(bf16[4,8,2,72,1152]{4,3,2,1,0:T(8,128)(2,1)} %get-tuple-element.123), kind=kLoop, calls=%fused_computation.178 | loop fusion | bytes 21233664 | tf_op jit(solution)/shard_map/slice | solution.py:663
  179.5 4.1 convolution_convert_fusion.15
  186.8 8.9 %all-to-all-done = bf16[3,128,1152]{1,0,2:T(4,128)(2,1)S(1)} async-done(((bf16[3,128,1152]{1,0,2:T(4,128)(2,1)}), bf16[3,128,1152]{1,0,2:T(4,128)(2,1)S(1)}, u32[]{:S(2)}, u32[]{:S(2)}) %all-to-all-start) | async-done | bytes 884768 | tf_op jit(solution)/shard_map/all_to_all | solution.py:588
  199.3 4.4 fusion.20
  206.9 7.7 %all-to-all-done.2 = bf16[3,128,1152]{1,0,2:T(4,128)(2,1)S(1)} async-done(((bf16[3,128,1152]{1,0,2:T(4,128)(2,1)}), bf16[3,128,1152]{1,0,2:T(4,128)(2,1)S(1)}, u32[]{:S(2)}, u32[]{:S(2)}) %all-to-all-start.2) | async-done | bytes 884768 | tf_op jit(solution)/shard_map/all_to_all | solution.py:588
  214.6 4.5 all-to-all-start.1
  221.6 12.2 %all-to-all-done.1 = bf16[3,128,1152]{1,0,2:T(4,128)(2,1)} async-done(((bf16[3,128,1152]{1,0,2:T(4,128)(2,1)}), bf16[3,128,1152]{1,0,2:T(4,128)(2,1)}, u32[]{:S(2)}, u32[]{:S(2)}) %all-to-all-start.1) | async-done | bytes 884768 | tf_op jit(solution)/shard_map/all_to_all | solution.py:588
  236.4 13.9 %while.26 = (s32[]{:T(128)}, bf16[3,512,288]{1,2,0:T(8,128)(2,1)}, f32[3,4,512]{2,1,0:T(4,128)}, bf16[3,512,288]{1,2,0:T(8,128)(2,1)S(1)}, pred[3,512]{1,0:T(4,1...) while((s32[]{:T(128)}, bf16[3,512,288]{1,2,0:T(8,128)(2,1)}, ...), condition=%wide.region_5.6_spmd, body=%wide.region_2.5_spmd.sunk | while | flops 313669632 | bytes 16190065 | solution.py:686
  253.6 4.3 all-to-all-start.3
  258.0 14.8 %fusion.61 = (bf16[1,8,2,72,1152]{4,3,2,1,0:T(8,128)(2,1)}, bf16[1,8,2,72,1152]{4,3,2,1,0:T(8,128)(2,1)}, bf16[1,8,2,72,1152]{4,3,2,1,0:T(8,128)(2,1)}, bf16[1,8...) fusion(bf16[4,8,2,72,1152]{4,3,2,1,0:T(8,128)(2,1)} %get-tuple-, ...), kind=kLoop, calls=%fused_computation.176 | loop fusion | bytes 42467328 | tf_op jit(solution)/shard_map/slice | solution.py:691
  291.5 3.5 copy.110
  369.1 4.3 all-to-all-start.4
  373.4 4.6 convolution_convert_fusion.6
  386.4 5.7 convolution_add_fusion.7
  397.5 28.0 %while.27 = (s32[]{:T(128)}, bf16[3,512,288]{1,2,0:T(8,128)(2,1)}, bf16[3,512,288]{1,2,0:T(8,128)(2,1)}, bf16[3,512,288]{1,2,0:T(8,128)(2,1)}, bf16[3,512,288]{1...) while((s32[]{:T(128)}, bf16[3,512,288]{1,2,0:T(8,128)(2,1)}, ...), condition=%wide.region_12.13_spmd, body=%wide.region_10.12_spmd.sunk | while | flops 767539200 | bytes 27183264 | solution.py:709
  428.9 4.5 all-to-all-start.5
  434.2 5.8 fusion.18
  444.6 7.7 %all-to-all-done.5 = bf16[3,512,288]{2,0,1:T(4,128)(2,1)} async-done(((bf16[3,512,288]{2,0,1:T(4,128)(2,1)}), bf16[3,512,288]{2,0,1:T(4,128)(2,1)}, u32[]{:S(2)}, u32[]{:S(2)}) %all-to-all-start.5) | async-done | bytes 884768 | tf_op jit(solution)/shard_map/all_to_all | solution.py:592
  452.3 3.7 all-to-all-start.6
  456.0 3.7 convert_reduce_fusion.1
  462.6 4.5 convolution_convert_fusion.13
  469.7 5.0 all-to-all-done.6
  475.9 3.6 all-to-all-start.7
  479.4 3.5 copy.109
  485.8 4.6 convolution_convert_fusion.12
  493.1 5.1 all-to-all-done.7
  510.0 183.6 %reduce_grads.1 = (bf16[4,2,72,1152]{3,2,1,0:T(8,128)(2,1)}, bf16[4,2,72,1152]{3,2,1,0:T(8,128)(2,1)}, bf16[4,2,72,1152]{3,2,1,0:T(8,128)(2,1)}, f32[16,128]{1,0:T(8,128)}) custom-call(bf16[8,1,2,72,1152]{4,3,2,1,0:T(8,128)(2,1)} %bitcast.360, bf16[8,1,2,72,1152]{4,3,2,1,0:T(8,128)(2,1)} %bitcast.367, bf16[8,1,2,72,1152]{4,3,2,1,0:T(8,128)(2,1)} %bitcast.368, ...), custom_call_target="tpu_custom_call" | custom-call | tf_op jit(solution)/shard_map/reduce_grads/pallas_call | solution.py:465
  699.4 4.5 reshape_reshape.12
  703.9 4.4 copy.108
  708.3 4.1 reshape.541
  714.2 4.3 reshape.548
  (346 shorter events, 242.7 us)
Async XLA Ops:
  16.4 142.1 %copy-start.2 = (bf16[3,128,1152]{2,1,0:T(8,128)(2,1)S(1)}, bf16[3,128,1152]{2,1,0:T(8,128)(2,1)}, u32[]{:S(2)}) copy-start(bf16[3,128,1152]{2,1,0:T(8,128)(2,1)} %param.22) | copy-start | bytes 2654212
  158.6 10.5 %copy-start.40 = (f32[1152]{0:T(1024)}, f32[1152]{0:T(1024)S(1)}, u32[]{:S(2)}) copy-start(f32[1152]{0:T(1024)S(1)} %mul.305) | copy-start | bytes 13828
  167.6 5.0 copy-start.12
  172.6 6.8 copy-start.28
  175.9 19.8 %all-to-all-start = ((bf16[3,128,1152]{1,0,2:T(4,128)(2,1)}), bf16[3,128,1152]{1,0,2:T(4,128)(2,1)S(1)}, u32[]{:S(2)}, u32[]{:S(2)}) async-start(bf16[3,128,1152]{1,0,2:T(4,128)(2,1)} %copy.68), calls=%async_computation | async-start | bytes 2359296 | tf_op jit(solution)/shard_map/all_to_all | solution.py:588
  183.5 15.7 %copy-start.48 = (f32[8,144]{1,0:T(8,128)S(1)}, f32[8,144]{1,0:T(8,128)}, u32[]{:S(2)}) copy-start(f32[8,144]{1,0:T(8,128)} %get-tuple-element.217) | copy-start | bytes 13828
  195.7 18.9 %all-to-all-start.2 = ((bf16[3,128,1152]{1,0,2:T(4,128)(2,1)}), bf16[3,128,1152]{1,0,2:T(4,128)(2,1)S(1)}, u32[]{:S(2)}, u32[]{:S(2)}) async-start(bf16[3,128,1152]{1,0,2:T(4,128)(2,1)} %copy.74), calls=%async_computation.2 | async-start | bytes 2359296 | tf_op jit(solution)/shard_map/all_to_all | solution.py:588
  203.7 15.4 %copy-start.56 = (s32[3,512]{1,0:T(4,128)S(1)}, s32[3,512]{1,0:T(4,128)}, u32[]{:S(2)}) copy-start(s32[3,512]{1,0:T(4,128)} %param.23) | copy-start | bytes 18436
  214.6 4.7 copy-start.6
  214.6 19.1 %all-to-all-start.1 = ((bf16[3,128,1152]{1,0,2:T(4,128)(2,1)}), bf16[3,128,1152]{1,0,2:T(4,128)(2,1)}, u32[]{:S(2)}, u32[]{:S(2)}) async-start(bf16[3,128,1152]{1,0,2:T(4,128)(2,1)} %copy.71), calls=%async_computation.1 | async-start | bytes 2359296 | tf_op jit(solution)/shard_map/all_to_all | solution.py:588
  253.6 37.9 %all-to-all-start.3 = ((bf16[3,512,288]{2,0,1:T(4,128)(2,1)}), bf16[3,512,288]{2,0,1:T(4,128)(2,1)}, u32[]{:S(2)}, u32[]{:S(2)}) async-start(bf16[3,512,288]{2,0,1:T(4,128)(2,1)} %copy.77), calls=%async_computation.3 | async-start | bytes 3145728 | tf_op jit(solution)/shard_map/all_to_all | solution.py:592
  258.0 17.6 %copy-start.47 = (f32[8,144]{1,0:T(8,128)S(1)}, f32[8,144]{1,0:T(8,128)}, u32[]{:S(2)}) copy-start(f32[8,144]{1,0:T(8,128)} %get-tuple-element.214) | copy-start | bytes 13828
  301.8 30.0 %copy-start = (f32[384,1152]{1,0:T(8,128)}, f32[384,1152]{1,0:T(8,128)S(1)}, u32[]{:S(2)}) copy-start(f32[384,1152]{1,0:T(8,128)S(1)} %get-tuple-element.234) | copy-start | bytes 5308420
  302.9 42.9 %copy-start.33 = (bf16[384,1152]{1,0:T(8,128)(2,1)}, bf16[384,1152]{1,0:T(8,128)(2,1)S(1)}, u32[]{:S(2)}) copy-start(bf16[384,1152]{1,0:T(8,128)(2,1)S(1)} %add_convert_fusion) | copy-start | bytes 2654212
  315.5 40.2 %copy-start.72 = (f32[384,1152]{1,0:T(8,128)}, f32[384,1152]{1,0:T(8,128)S(1)}, u32[]{:S(2)}) copy-start(f32[384,1152]{1,0:T(8,128)S(1)} %convolution_add_fusion.8) | copy-start | bytes 5308420
  317.3 41.9 %copy-start.75 = (f32[384,1152]{1,0:T(8,128)}, f32[384,1152]{1,0:T(8,128)S(1)}, u32[]{:S(2)}) copy-start(f32[384,1152]{1,0:T(8,128)S(1)} %convolution_add_fusion.6) | copy-start | bytes 5308420
  369.1 23.0 %all-to-all-start.4 = ((bf16[3,128,1152]{1,0,2:T(4,128)(2,1)}), bf16[3,128,1152]{1,0,2:T(4,128)(2,1)}, u32[]{:S(2)}, u32[]{:S(2)}) async-start(bf16[3,128,1152]{1,0,2:T(4,128)(2,1)} %copy.79), calls=%async_computation.4 | async-start | bytes 2359296 | tf_op jit(solution)/shard_map/all_to_all | solution.py:588
  373.4 4.6 copy-start.43
  428.9 4.5 copy-start.49
  428.9 4.5 copy-start.50
  428.9 4.5 copy-start.51
  428.9 4.6 copy-start.52
  428.9 5.3 copy-start.1
  428.9 23.4 %all-to-all-start.5 = ((bf16[3,512,288]{2,0,1:T(4,128)(2,1)}), bf16[3,512,288]{2,0,1:T(4,128)(2,1)}, u32[]{:S(2)}, u32[]{:S(2)}) async-start(bf16[3,512,288]{2,0,1:T(4,128)(2,1)} %copy.82), calls=%async_computation.5 | async-start | bytes 3145728 | tf_op jit(solution)/shard_map/all_to_all | solution.py:592
  434.2 5.8 copy-start.10
  452.3 22.5 %all-to-all-start.6 = ((bf16[3,512,288]{2,0,1:T(4,128)(2,1)}), bf16[3,512,288]{2,0,1:T(4,128)(2,1)S(1)}, u32[]{:S(2)}, u32[]{:S(2)}) async-start(bf16[3,512,288]{2,0,1:T(4,128)(2,1)} %copy.84), calls=%async_computation.6 | async-start | bytes 3145728 | tf_op jit(solution)/shard_map/all_to_all | solution.py:592
  456.0 6.6 copy-start.29
  462.6 4.5 copy-start.32
  475.9 22.3 %all-to-all-start.7 = ((bf16[3,512,288]{2,0,1:T(4,128)(2,1)}), bf16[3,512,288]{2,0,1:T(4,128)(2,1)S(1)}, u32[]{:S(2)}, u32[]{:S(2)}) async-start(bf16[3,512,288]{2,0,1:T(4,128)(2,1)} %copy.86), calls=%async_computation.7 | async-start | bytes 3145728 | tf_op jit(solution)/shard_map/all_to_all | solution.py:592
  485.8 4.6 copy-start.14
  485.8 4.6 copy-start.31
  485.8 4.6 copy-start.74
  (52 other events, 128.9 us)

commit v2 on v0

v2 whole, which is shorter than its diff:
```python
import functools

import jax
import jax.numpy as jnp
from jax import lax
from jax.experimental import pallas as pl
from jax.experimental.pallas import tpu as pltpu
from jax.sharding import PartitionSpec as P

HD = 72
EPSILON = 1e-06
MASKED = -1e30
LOG2_E = 1.4426950408889634
MESH = pl.DeviceIdType.MESH
VMEM_LIMIT = 64_000_000
BLOCKS = 4
LOW = jnp.bfloat16
WIDE = jnp.float32


def wide(values):
    return values.astype(WIDE)


def product(left, right):
    return jnp.dot(left, right, preferred_element_type=WIDE)


def product_rows(left, right):
    return lax.dot_general(left, right, (((0,), (0,)), ((), ())), preferred_element_type=WIDE)


def product_back(left, right):
    return lax.dot_general(left, right, (((1,), (1,)), ((), ())), preferred_element_type=WIDE)


def flip(index, bit):
    on = lax.rem(lax.div(index, 1 << bit), 2)
    return index + (1 - 2 * on) * (1 << bit)


def flip_mask(index, mask):
    bit = 0
    while mask >> bit:
        if (mask >> bit) & 1:
            index = flip(index, bit)
        bit += 1
    return index


PLAN = (((0, (0,), 0), (1, (0, 1), 1)), ((1, (0,), 0), (0, (0, 2), 1)))


class Place:
    def __init__(self, n_seq, n_fsdp, depth):
        self.n_seq, self.n_fsdp, self.depth = n_seq, n_fsdp, depth
        self.n_z = n_fsdp // 2
        self.s, self.f = lax.axis_index("seq"), lax.axis_index("fsdp")
        self.core, self.z = lax.rem(self.f, 2), lax.div(self.f, 2)
        self.block = lax.rem(self.s, BLOCKS)
        self.other = self.f + 1 - 2 * self.core
        n_z = self.n_z
        self.to_f = [lax.rem(self.z + d, n_z) * 2 + self.core for d in range(n_z)]
        self.from_f = [lax.rem(self.z - d + n_z, n_z) * 2 + self.core for d in range(n_z)]
        self.to_s = [lax.rem(self.s + d, n_seq) for d in range(n_seq)]
        self.from_s = [lax.rem(self.s - d + n_seq, n_seq) for d in range(n_seq)]
        first = depth // 32 * 16
        self.halves = ((0, first), (first, depth - first))
        self.sent = []

    def greet(self):
        barrier = pltpu.get_barrier_semaphore()
        peers = [(self.s, self.other)]
        peers += [(self.s, f) for f in self.to_f[1:]]
        peers += [(s, self.f) for s in self.to_s[1:]]
        for s, f in peers:
            pl.semaphore_signal(
                barrier, inc=1, device_id={"seq": s, "fsdp": f}, device_id_type=MESH
            )
        pl.semaphore_wait(barrier, len(peers))

    def copy(self, src, dst, sems, index, s, f):
        return pltpu.make_async_remote_copy(
            src_ref=src,
            dst_ref=dst,
            send_sem=sems[0].at[index],
            recv_sem=sems[1].at[index],
            device_id={"seq": s, "fsdp": f},
            device_id_type=MESH,
        )

    def start(self, copies):
        for copy in copies:
            copy.start()
            self.sent.append(copy)

    def finish(self):
        for copy in self.sent:
            copy.wait_send()

    def rows(self, f, half=None):
        offset, size = (0, self.depth) if half is None else self.halves[half]
        return pl.ds(pl.multiple_of(f * self.depth + offset, 8), size)

    def part(self, half):
        return pl.ds(*self.halves[half])


def arrive(copies):
    for copy in copies:
        copy.wait_recv()


class Exchange:
    def __init__(self, place, out, into, sems, local):
        self.place, self.out, self.into, self.sems, self.local = place, out, into, sems, local

    def send(self, i):
        at = self.place
        at.start(
            at.copy(
                self.out.at[i, at.to_s[d]],
                self.into.at[i, at.s],
                self.sems,
                (i, d),
                at.to_s[d],
                at.f,
            )
            for d in range(1, at.n_seq)
        )
        self.keep(i).start()

    def keep(self, i):
        at = self.place
        return pltpu.make_async_copy(
            self.out.at[i, at.s], self.into.at[i, at.s], self.local.at[i]
        )

    def receive(self, i):
        at = self.place
        arrive(
            at.copy(
                self.out.at[i, at.to_s[d]],
                self.into.at[i, at.from_s[d]],
                self.sems,
                (i, d),
                at.to_s[d],
                at.f,
            )
            for d in range(1, at.n_seq)
        )
        self.keep(i).wait()


def heads_of(ref, i, w, head, n_seq):
    rows = slice(head * HD, (head + 1) * HD)
    return jnp.concatenate([ref[i, t, w, rows, :] for t in range(n_seq)], axis=1)


def normalize(values):
    center = values - jnp.mean(values, axis=-1, keepdims=True)
    factor = lax.rsqrt(jnp.mean(center * center, axis=-1, keepdims=True) + EPSILON)
    return (center * factor, factor)


def forward_heads(i, heads, n_seq, qkv, mask, logsum):
    scale = HD ** (-0.5) * LOG2_E
    outs, sums = [], []
    for h in range(heads):
        query, keys, values = (heads_of(qkv, i, w, h, n_seq) for w in range(3))
        scores = product_rows(keys, query) + mask[i]
        highest = jnp.max(scores, axis=0, keepdims=True)
        weights = jnp.exp2((scores - highest) * scale)
        total = jnp.sum(weights, axis=0, keepdims=True)
        outs.append(product(values, (weights * (1.0 / total)).astype(LOW)))
        sums.append(highest * scale + jnp.log2(total))
    logsum[i] = jnp.concatenate(sums, axis=0)
    return jnp.concatenate(outs, axis=0)


def backward_heads(i, heads, n_seq, qkv, attended, grad, mask, logsum):
    scale = HD ** (-0.5)
    grads = [[], [], []]
    for h in range(heads):
        query, keys, values = (heads_of(qkv, i, w, h, n_seq) for w in range(3))
        grad_out = heads_of(grad, i, 0, h, n_seq)
        delta = jnp.sum(
            wide(grad_out) * wide(heads_of(attended, i, 0, h, n_seq)), axis=0, keepdims=True
        )
        scores = product_rows(keys, query) * (scale * LOG2_E)
        chance = jnp.exp2(scores + mask[i] - logsum[i, h : h + 1, :])
        grad_scores = chance * (product_rows(values, grad_out) - delta) * scale
        grads[2].append(product_back(grad_out, chance.astype(LOW)))
        grad_scores = grad_scores.astype(LOW)
        grads[0].append(product(keys, grad_scores))
        grads[1].append(product_back(query, grad_scores))
    return [jnp.concatenate(item, axis=0) for item in grads]


def scatter_tokens(value, n_seq, out, i, w):
    block = value.shape[1] // n_seq
    low = value.astype(LOW)
    for t in range(n_seq):
        out[i, t, w] = low[:, t * block : (t + 1) * block]


def forward_kernel(n_seq, n_fsdp, packs, *refs):
    refs = list(refs)

    def take(n):
        items = refs[:n]
        del refs[:n]
        return items

    images, mask, vec = take(3)
    own = take(packs)
    full = take(packs)
    vec_rows, hidden, attended_flat, logsum, qkv_out, attended_out = take(6)
    weight, vec_full, spread, qkv, attended, attended_in = take(6)
    z_sems, p_sems, c_sems, v_sems, a_sems, b_sems = (take(2) for _ in range(6))
    local, load, a_local, b_local, o_sem = take(5)
    count, block, width = images.shape
    depth = own[0].shape[1]
    group = width // n_seq
    heads = group // HD
    at = Place(n_seq, n_fsdp, depth)
    n_z = at.n_z
    at.greet()

    def vec_copy(src, dst, sem, f):
        return at.copy(src, vec_full.at[dst], v_sems, sem, at.s, f)

    def z_copy(p, d, arriving):
        dst = full[p].at[at.block, at.rows(at.from_f[d] if arriving else at.f)]
        return at.copy(own[p].at[at.block], dst, z_sems, (p, d), at.s, at.to_f[d])

    def plane(p, d, k, arriving):
        for half, steps in enumerate(PLAN):
            bit, masks, slot = steps[k]
            rows = at.rows(at.from_f[d], half)
            for i, m in enumerate(masks):
                src = full[p].at[flip_mask(at.block, m), rows]
                dst = full[p].at[flip_mask(at.block, m ^ (1 << bit)), rows] if arriving else src
                yield at.copy(src, dst, p_sems, (p, d, half, slot + i), flip(at.s, bit), at.f)

    def core_copy(p, d, arriving):
        f = at.from_f[d]
        src = own[p] if d == 0 else full[p].at[:, at.rows(f)]
        dst = full[p].at[:, at.rows(f + 1 - 2 * at.core if arriving else f)]
        return at.copy(src, dst, c_sems, (p, d), at.s, at.other)

    at.start([vec_copy(vec, at.f, d, at.to_f[d]) for d in range(1, n_z)])
    at.start([vec_copy(vec, at.f, 0, at.other)])
    at.start([z_copy(p, d, False) for p in range(packs) for d in range(1, n_z)])
    keep = [
        pltpu.make_async_copy(own[p], full[p].at[:, at.rows(at.f)], local.at[p])
        for p in range(packs)
    ] + [pltpu.make_async_copy(vec, vec_full.at[at.f], local.at[packs])]
    for copy in keep:
        copy.start()
    at.start([core_copy(p, 0, False) for p in range(packs)])
    for d in range(1, n_z):
        arrive([vec_copy(vec, at.from_f[d], d, at.to_f[d])])
        at.start([vec_copy(vec_full.at[at.from_f[d]], at.from_f[d], n_z - 1 + d, at.other)])
    for d in range(n_z):
        sem = n_z - 1 + d if d else 0
        f = at.from_f[d] + 1 - 2 * at.core
        arrive([vec_copy(vec_full.at[f], f, sem, at.other)])
    keep[packs].wait()

    vec_rows[...] = jnp.concatenate([wide(vec_full[f]) for f in range(n_fsdp)], axis=1)
    for i in range(count):
        normed, _ = normalize(wide(images[i]))
        rows = slice(i * block, (i + 1) * block)
        hidden[rows, :] = (normed * vec_rows[0:1, :] + vec_rows[1:2, :]).astype(LOW)

    def from_z(p, d):
        arrive([z_copy(p, d, True)])
        at.start(plane(p, d, 0, False))

    def second_step(p):
        for d in range(1, n_z):
            arrive(plane(p, d, 0, True))
            at.start(plane(p, d, 1, False))

    def to_core(p, d):
        arrive(plane(p, d, 1, True))
        at.start([core_copy(p, d, False)])

    def weight_load(w):
        return pltpu.make_async_copy(full[0].at[w], weight.at[w % 2], load.at[w % 2])

    send_heads = Exchange(at, spread, qkv, a_sems, a_local)
    send_tokens = Exchange(at, attended, attended_in, b_sems, b_local)

    for d in range(1, n_z):
        from_z(0, d)
    second_step(0)
    for d in range(1, n_z):
        from_z(1, d)
        to_core(0, d)
    for d in range(n_z):
        arrive([core_copy(0, d, True)])
    keep[0].wait()
    weight_load(0).start()
    for w in range(3):
        if w < 2:
            weight_load(w + 1).start()
        weight_load(w).wait()
        value = product(hidden[...], weight[w % 2])
        if w != 1:
            value = value + vec_rows[2 + w // 2 : 3 + w // 2, :]
        value = value.T.astype(LOW)
        for i in range(count):
            for t in range(n_seq):
                spread[i, t, w] = value[
                    t * group : (t + 1) * group, i * block : (i + 1) * block
                ]
    for i in range(count):
        send_heads.send(i)
    second_step(1)
    for d in range(1, n_z):
        from_z(2, d)
    for i in range(count):
        send_heads.receive(i)
        scatter_tokens(
            forward_heads(i, heads, n_seq, qkv, mask, logsum), n_seq, attended, i, 0
        )
        send_tokens.send(i)
        if i == 0:
            for d in range(1, n_z):
                to_core(1, d)
            second_step(2)
    saves = [
        pltpu.make_async_copy(qkv, qkv_out, o_sem.at[0]),
        pltpu.make_async_copy(attended, attended_out, o_sem.at[1]),
    ]
    for copy in saves:
        copy.start()
    for d in range(1, n_z):
        to_core(2, d)
    for i in range(count):
        send_tokens.receive(i)
        features = jnp.concatenate([attended_in[i, t, 0] for t in range(n_seq)], axis=0)
        attended_flat[i * block : (i + 1) * block, :] = wide(features).T.astype(LOW)
    for p in range(packs):
        if p > 0:
            keep[p].wait()
            for d in range(n_z):
                arrive([core_copy(p, d, True)])
    for copy in saves:
        copy.wait()
    at.finish()


def forward_all(n_seq, n_fsdp, images, mask, vec, packed):
    packs = len(packed)
    count, block, width = images.shape
    length = mask.shape[1]
    n_z, group = n_fsdp // 2, width // n_seq
    heads = group // HD
    dma, vmem, any_space = pltpu.SemaphoreType.DMA, pltpu.VMEM, pl.BlockSpec(memory_space=pl.ANY)
    in_vmem = pl.BlockSpec(memory_space=pltpu.VMEM)
    shape = jax.ShapeDtypeStruct
    qkv = (count, n_seq, 3, group, block)
    att = (count, n_seq, 1, group, block)
    pair = lambda *dims: [dma(dims), dma(dims)]
    return pl.pallas_call(
        functools.partial(forward_kernel, n_seq, n_fsdp, packs),
        out_shape=[shape((BLOCKS, width, width), LOW) for _ in range(packs)]
        + [
            shape((vec.shape[0], width), WIDE),
            shape((count * block, width), LOW),
            shape((count * block, width), LOW),
            shape((count, heads, length), WIDE),
            shape(qkv, LOW),
            shape(att, LOW),
        ],
        in_specs=[in_vmem] * (3 + packs),
        out_specs=[any_space] * packs + [in_vmem] * 4 + [any_space] * 2,
        scratch_shapes=[
            vmem((2, width, width), LOW),
            vmem((n_fsdp,) + vec.shape, LOW),
            vmem(qkv, LOW),
            vmem(qkv, LOW),
            vmem(att, LOW),
            vmem(att, LOW),
            *pair(packs, n_z),
            *pair(packs, n_z, 2, BLOCKS - 1),
            *pair(packs, n_z),
            *pair(2 * n_z - 1),
            *pair(count, n_seq),
            *pair(count, n_seq),
            dma((packs + 1,)),
            dma((2,)),
            dma((count,)),
            dma((count,)),
            dma((2,)),
        ],
        compiler_params=pltpu.CompilerParams(
            collective_id=0, has_side_effects=True, vmem_limit_bytes=VMEM_LIMIT
        ),
        name="forward_attention",
    )(images, mask, vec, *packed)


def add_rows(target, term, start, size):
    step = 16 if start % 16 == 0 and size % 16 == 0 else 8

    def body(i, _):
        rows = pl.ds(pl.multiple_of(start + i * step, step), step)
        target[rows, :] = (wide(target[rows, :]) + wide(term[rows, :])).astype(LOW)
        return 0

    lax.fori_loop(0, size // step, body, 0)


class Reduction:
    SCRATCH = 14

    @staticmethod
    def scratch(n_seq, n_fsdp, packs, depth, width):
        n_z, upper = n_fsdp // 2, n_seq.bit_length() - 3
        dma, vmem = pltpu.SemaphoreType.DMA, pltpu.VMEM
        piece = (depth, width)
        pair = lambda *dims: [dma(dims), dma(dims)]
        return [
            vmem((packs, n_z, BLOCKS) + piece, LOW),
            vmem((packs, n_z, BLOCKS) + piece, LOW),
            vmem((packs, n_z, BLOCKS - 1) + piece, LOW),
            vmem((packs, n_z - 1) + piece, LOW),
            vmem((packs, BLOCKS) + piece, LOW),
            vmem((max(upper, 1), packs, n_z, BLOCKS) + (piece if upper else (8, 128)), LOW),
            dma((packs, n_z, BLOCKS)),
            dma((packs,)),
            *pair(packs, n_z, BLOCKS),
            *pair(packs, n_z, 2, BLOCKS - 1),
            *pair(packs, n_z),
            *pair(packs, 2, BLOCKS - 1),
            *pair(max(upper, 1), packs, n_z),
        ]

    def __init__(self, at, packs, grads, out, scratch):
        self.at, self.packs, self.grads, self.out = at, packs, grads, out
        (
            self.held,
            self.core_in,
            self.plane_in,
            self.z_in,
            self.total,
            self.upper_in,
            self.load_sem,
            self.out_sem,
            *sems,
        ) = scratch
        self.c_sems, self.p_sems, self.z_sems, self.g_sems, self.u_sems = (
            sems[2 * i : 2 * i + 2] for i in range(5)
        )
        self.upper = at.n_seq.bit_length() - 3

    def target_z(self, t):
        return lax.rem(self.at.z + t + 1, self.at.n_z)

    def load(self, p, t):
        rows = self.at.rows(2 * self.target_z(t) + self.at.core)
        return [
            pltpu.make_async_copy(
                self.grads[p][q].at[rows], self.held.at[p, t, q], self.load_sem.at[p, t, q]
            )
            for q in range(BLOCKS)
        ]

    def to_partner(self, p, t):
        at = self.at
        rows = at.rows(2 * self.target_z(t) + 1 - at.core)
        return [
            at.copy(
                self.grads[p][q].at[rows],
                self.core_in.at[p, t, q],
                self.c_sems,
                (p, t, q),
                at.s,
                at.other,
            )
            for q in range(BLOCKS)
        ]

    def start(self, p, t):
        self.at.start(self.to_partner(p, t))
        for copy in self.load(p, t):
            copy.start()

    def plane(self, p, t, k):
        at = self.at
        for half, steps in enumerate(PLAN):
            bit, masks, slot = steps[k]
            for i, m in enumerate(masks):
                src = self.held.at[p, t, flip_mask(at.block, m ^ (1 << bit)), at.part(half)]
                dst = self.plane_in.at[p, t, slot + i, at.part(half)]
                yield at.copy(
                    src, dst, self.p_sems, (p, t, half, slot + i), flip(at.s, bit), at.f
                )

    def z_copy(self, p, t):
        at = self.at
        return at.copy(
            self.held.at[p, t, at.block],
            self.z_in.at[p, t],
            self.z_sems,
            (p, t),
            at.s,
            2 * self.target_z(t) + at.core,
        )

    def up_copy(self, u, p, t):
        at = self.at
        return at.copy(
            self.held.at[p, t],
            self.upper_in.at[u, p, t],
            self.u_sems,
            (u, p, t),
            flip(at.s, 2 + u),
            at.f,
        )

    def spread(self, p, k, arriving):
        at = self.at
        for half, steps in enumerate(PLAN):
            bit, masks, slot = steps[k]
            for i, m in enumerate(masks):
                src = self.total.at[p, flip_mask(at.block, m), at.part(half)]
                dst = self.total.at[p, flip_mask(at.block, m ^ (1 << bit)), at.part(half)]
                yield at.copy(
                    src,
                    dst if arriving else src,
                    self.g_sems,
                    (p, half, slot + i),
                    flip(at.s, bit),
                    at.f,
                )

    def stage_core(self, p, t):
        for copy in self.load(p, t):
            copy.wait()
        arrive(self.to_partner(p, t))

        def body(q, _):
            add_rows(self.held.at[p, t, q], self.core_in.at[p, t, q], 0, self.at.depth)
            return 0

        lax.fori_loop(0, BLOCKS, body, 0)
        for u in range(self.upper):
            copy = self.up_copy(u, p, t)
            copy.start()
            copy.wait()

            def upper_body(q, _, u=u):
                add_rows(self.held.at[p, t, q], self.upper_in.at[u, p, t, q], 0, self.at.depth)
                return 0

            lax.fori_loop(0, BLOCKS, upper_body, 0)
        self.at.start(self.plane(p, t, 1))

    def stage_plane(self, p, t, k):
        arrive(self.plane(p, t, k))
        for half, steps in enumerate(PLAN):
            _, masks, slot = steps[k]
            for i, m in enumerate(masks):
                add_rows(
                    self.held.at[p, t, flip_mask(self.at.block, m)],
                    self.plane_in.at[p, t, slot + i],
                    *self.at.halves[half],
                )
        if k > 0:
            self.at.start(self.plane(p, t, k - 1))
        elif t < self.at.n_z - 1:
            self.at.start([self.z_copy(p, t)])

    def stage_total(self, p):
        last = self.at.n_z - 1
        arrive(self.z_copy(p, t) for t in range(last))
        step = 16 if self.at.depth % 16 == 0 else 8

        def body(i, _):
            rows = pl.ds(pl.multiple_of(i * step, step), step)
            value = wide(self.held[p, last, self.at.block, rows, :])
            for t in range(last):
                value = value + wide(self.z_in[p, t, rows, :])
            self.total[p, self.at.block, rows, :] = value.astype(LOW)
            return 0

        lax.fori_loop(0, self.at.depth // step, body, 0)
        self.at.start(self.spread(p, 0, False))

    def stage_spread(self, p, k):
        arrive(self.spread(p, k - 1, True))
        if k < 2:
            self.at.start(self.spread(p, k, False))
        else:
            self.save(p).start()

    def save(self, p):
        return pltpu.make_async_copy(self.total.at[p], self.out[p], self.out_sem.at[p])

    def events(self):
        n_z, out = self.at.n_z, []
        for i, (p, t) in enumerate((p, t) for p in range(self.packs) for t in range(n_z)):
            out.append((i, 0, functools.partial(self.stage_core, p, t)))
            out.append((i + 1, 1, functools.partial(self.stage_plane, p, t, 1)))
            out.append((i + 2, 2, functools.partial(self.stage_plane, p, t, 0)))
        for p in range(self.packs):
            last = (p + 1) * n_z + 1
            out.append((last + 1.5, 3, functools.partial(self.stage_total, p)))
            out.append((last + 2.5, 4, functools.partial(self.stage_spread, p, 1)))
            out.append((last + 3.5, 5, functools.partial(self.stage_spread, p, 2)))
        return out

    def finish(self):
        for p in range(self.packs):
            self.save(p).wait()


def run_events(events):
    for _, _, call in sorted(events, key=lambda e: e[:2]):
        call()


def backward_kernel(n_seq, n_fsdp, packs, *refs):
    refs = list(refs)

    def take(n):
        items = refs[:n]
        del refs[:n]
        return items

    grads = [take(BLOCKS) for _ in range(packs)]
    grad_flat, mask, logsum, qkv, attended = take(5)
    out = take(packs)
    (grad_out,) = take(1)
    grad_spread, grad_heads, back_spread, back_in = take(4)
    a_sems, b_sems = take(2), take(2)
    a_local, b_local = take(2)
    count, _, _, group, block = qkv.shape
    width = grad_flat.shape[1]
    heads = group // HD
    at = Place(n_seq, n_fsdp, width // n_fsdp)
    reduction = Reduction(at, packs, grads, out, refs)
    at.greet()
    send_heads = Exchange(at, grad_spread, grad_heads, a_sems, a_local)
    send_tokens = Exchange(at, back_spread, back_in, b_sems, b_local)
    for i in range(count):
        value = wide(grad_flat[i * block : (i + 1) * block, :]).T.astype(LOW)
        for t in range(n_seq):
            grad_spread[i, t, 0] = value[t * group : (t + 1) * group]
        send_heads.send(i)
    for p in range(packs):
        for t in range(at.n_z):
            reduction.start(p, t)

    def image(i):
        send_heads.receive(i)
        for w, value in enumerate(
            backward_heads(i, heads, n_seq, qkv, attended, grad_heads, mask, logsum)
        ):
            scatter_tokens(value, n_seq, back_spread, i, w)
        send_tokens.send(i)

    def collect(i):
        send_tokens.receive(i)
        for w in range(3):
            features = jnp.concatenate([back_in[i, t, w] for t in range(n_seq)], axis=0)
            grad_out[w, i * block : (i + 1) * block, :] = wide(features).T.astype(LOW)

    events = reduction.events()
    for i in range(count):
        events.append((1 + i, 10, functools.partial(image, i)))
        events.append((5 + i, 11, functools.partial(collect, i)))
    run_events(events)
    reduction.finish()
    at.finish()


def backward_all(n_seq, n_fsdp, squares, grad_flat, mask, logsum, qkv, attended):
    packs = len(squares) // BLOCKS
    width = grad_flat.shape[1]
    depth = width // n_fsdp
    count = qkv.shape[0]
    any_space = pl.BlockSpec(memory_space=pl.ANY)
    in_vmem = pl.BlockSpec(memory_space=pltpu.VMEM)
    dma, vmem, shape = pltpu.SemaphoreType.DMA, pltpu.VMEM, jax.ShapeDtypeStruct
    pair = lambda *dims: [dma(dims), dma(dims)]
    return pl.pallas_call(
        functools.partial(backward_kernel, n_seq, n_fsdp, packs),
        out_shape=[shape((BLOCKS, depth, width), LOW) for _ in range(packs)]
        + [shape((3,) + grad_flat.shape, LOW)],
        in_specs=[any_space] * len(squares) + [in_vmem] * 5,
        out_specs=[any_space] * packs + [in_vmem],
        scratch_shapes=[
            vmem(attended.shape, LOW),
            vmem(attended.shape, LOW),
            vmem(qkv.shape, LOW),
            vmem(qkv.shape, LOW),
            *pair(count, n_seq),
            *pair(count, n_seq),
            dma((count,)),
            dma((count,)),
            *Reduction.scratch(n_seq, n_fsdp, packs, depth, width),
        ],
        compiler_params=pltpu.CompilerParams(
            collective_id=1, has_side_effects=True, vmem_limit_bytes=VMEM_LIMIT
        ),
        name="backward_attention",
    )(*squares, grad_flat, mask, logsum, qkv, attended)


def reduce_kernel(n_seq, n_fsdp, packs, *refs):
    refs = list(refs)

    def take(n):
        items = refs[:n]
        del refs[:n]
        return items

    grads = [take(BLOCKS) for _ in range(packs)]
    (vec,) = take(1)
    out = take(packs)
    (vec_out,) = take(1)
    work, came, z_came = take(3)
    v_sems = take(2)
    width = vec.shape[1]
    depth = width // n_fsdp
    at = Place(n_seq, n_fsdp, depth)
    n_z, bits = at.n_z, n_seq.bit_length() - 1
    reduction = Reduction(at, packs, grads, out, refs)
    at.greet()

    def vec_copy(i):
        src = vec if i == 0 else work.at[i - 1]
        peer = (at.s, at.other) if i == 0 else (flip(at.s, i - 1), at.f)
        return at.copy(src, came.at[i], v_sems, i, *peer)

    def vec_z(d):
        return at.copy(
            work.at[bits], z_came.at[lax.rem(at.z, n_z)], v_sems, bits + d, at.s, at.to_f[d]
        )

    def vec_stage(i):
        arrive([vec_copy(i)])
        work[i] = (vec[...] if i == 0 else work[i - 1]) + came[i]
        if i < bits:
            at.start([vec_copy(i + 1)])
        else:
            at.start([vec_z(d) for d in range(1, n_z)])

    def vec_last():
        for d in range(1, n_z):
            arrive(
                [
                    at.copy(
                        work.at[bits],
                        z_came.at[lax.div(at.from_f[d], 2)],
                        v_sems,
                        bits + d,
                        at.s,
                        at.to_f[d],
                    )
                ]
            )
        value = work[bits]
        for d in range(1, n_z):
            value = value + z_came[lax.div(at.from_f[d], 2)]
        for f in range(n_fsdp):

            @pl.when(at.f == f)
            def _(f=f):
                vec_out[...] = value[:, f * depth : (f + 1) * depth]

    at.start([vec_copy(0)])
    for p in range(packs):
        for t in range(n_z):
            reduction.start(p, t)
    events = reduction.events()
    for i in range(bits + 1):
        events.append((i, 20, functools.partial(vec_stage, i)))
    events.append((bits + 1, 20, vec_last))
    run_events(events)
    reduction.finish()
    at.finish()


def reduce_all(n_seq, n_fsdp, squares, vec):
    packs = len(squares) // BLOCKS
    width = vec.shape[1]
    depth = width // n_fsdp
    n_z, bits = n_fsdp // 2, n_seq.bit_length() - 1
    any_space = pl.BlockSpec(memory_space=pl.ANY)
    in_vmem = pl.BlockSpec(memory_space=pltpu.VMEM)
    dma, vmem, shape = pltpu.SemaphoreType.DMA, pltpu.VMEM, jax.ShapeDtypeStruct
    return pl.pallas_call(
        functools.partial(reduce_kernel, n_seq, n_fsdp, packs),
        out_shape=[shape((BLOCKS, depth, width), LOW) for _ in range(packs)]
        + [shape((vec.shape[0], depth), WIDE)],
        in_specs=[any_space] * len(squares) + [in_vmem],
        out_specs=[any_space] * packs + [in_vmem],
        scratch_shapes=[
            vmem((bits + 1,) + vec.shape, WIDE),
            vmem((bits + 1,) + vec.shape, WIDE),
            vmem((n_z,) + vec.shape, WIDE),
            dma((bits + n_z,)),
            dma((bits + n_z,)),
            *Reduction.scratch(n_seq, n_fsdp, packs, depth, width),
        ],
        compiler_params=pltpu.CompilerParams(
            collective_id=2, has_side_effects=True, vmem_limit_bytes=VMEM_LIMIT
        ),
        name="reduce_grads",
    )(*squares, vec)


def gelu_tanh(values):
    return jax.nn.gelu(values, approximate=True)


def norm_back(grad_normed, normed, factor):
    first = jnp.mean(grad_normed, axis=-1, keepdims=True)
    second = jnp.mean(grad_normed * normed, axis=-1, keepdims=True)
    return factor * (grad_normed - first - normed * second)


def shards(
    n_seq,
    n_fsdp,
    images,
    key_mask,
    attn_gain,
    attn_shift,
    query_weight,
    key_weight,
    value_weight,
    query_bias,
    value_bias,
    out_weight,
    out_bias,
    mlp_gain,
    mlp_shift,
    inner_weight,
    inner_bias,
    outer_weight,
    outer_bias,
    cotangent,
):
    count, block_len, width = images.shape
    rows = count * block_len
    depth = query_weight.shape[0]
    ff_own = outer_weight.shape[0]
    slack = BLOCKS * depth - ff_own

    inner_cols = jnp.pad(
        inner_weight.reshape(depth, n_fsdp, ff_own), ((0, 0), (0, 0), (0, slack))
    ).reshape(depth, n_fsdp, BLOCKS, depth)
    packed = (
        jnp.stack((query_weight, key_weight, value_weight, out_weight)),
        inner_cols.transpose(2, 0, 1, 3).reshape(BLOCKS, depth, width),
        jnp.pad(outer_weight, ((0, slack), (0, 0))).reshape(BLOCKS, depth, width),
    )
    small = [
        attn_gain,
        attn_shift,
        query_bias,
        value_bias,
        out_bias,
        mlp_gain,
        mlp_shift,
        outer_bias,
    ]
    vec = jnp.concatenate(
        [item.reshape(1, depth) for item in small]
        + [jnp.pad(inner_bias, (0, slack + BLOCKS * depth)).reshape(2 * BLOCKS, depth)]
    )
    mask = jnp.where(key_mask > 0, 0.0, MASKED).astype(WIDE)[:, :, None]
    *full, vecs, hidden_one, attended_flat, logsum, qkv, attended = forward_all(
        n_seq, n_fsdp, images, mask, vec, packed
    )
    w_attn, w_inner, w_outer = full
    w_query, w_key, w_value, w_out = (w_attn[i] for i in range(BLOCKS))
    gain_attn, _, _, _, b_out, gain_mlp, shift_mlp, b_outer = (vecs[i] for i in range(8))
    b_inner = [vecs[8 + i] for i in range(BLOCKS)]

    flat = wide(images.reshape(rows, width))
    second = flat + product(attended_flat, w_out) + b_out
    normed_two, factor_two = normalize(second)
    hidden_two = (normed_two * gain_mlp + shift_mlp).astype(LOW)
    inner = [product(hidden_two, w_inner[i]) + b_inner[i] for i in range(BLOCKS)]
    active = [gelu_tanh(item).astype(LOW) for item in inner]
    outer = sum(product(active[i], w_outer[i]) for i in range(BLOCKS))
    layer_out = second + outer + b_outer

    upstream = cotangent.reshape(rows, width)
    grad_inner = [
        jax.vjp(gelu_tanh, inner[i])[1](product_back(upstream, w_outer[i]))[0]
        for i in range(BLOCKS)
    ]
    grad_inner_low = [item.astype(LOW) for item in grad_inner]
    grad_hidden_two = sum(product_back(grad_inner_low[i], w_inner[i]) for i in range(BLOCKS))
    grad_second = wide(upstream) + norm_back(grad_hidden_two * gain_mlp, normed_two, factor_two)
    grad_second_low = grad_second.astype(LOW)

    grad_attended = product_back(grad_second_low, w_out).astype(LOW)
    mlp_squares = [product_rows(item, upstream).astype(LOW) for item in active]
    mlp_squares += [product_rows(hidden_two, item).astype(LOW) for item in grad_inner_low]
    sum_outer, sum_inner, grad_qkv = backward_all(
        n_seq, n_fsdp, mlp_squares, grad_attended, mask, logsum, qkv, attended
    )
    grad_query, grad_keys, grad_values = (grad_qkv[i] for i in range(3))
    grad_hidden_one = (
        product_back(grad_query, w_query)
        + product_back(grad_keys, w_key)
        + product_back(grad_values, w_value)
    )
    normed_one, factor_one = normalize(flat)
    images_grad = grad_second + norm_back(grad_hidden_one * gain_attn, normed_one, factor_one)

    squares = [
        product_rows(hidden_one, grad_query),
        product_rows(hidden_one, grad_keys),
        product_rows(hidden_one, grad_values),
        product_rows(attended_flat, grad_second_low),
    ]
    sums = [
        jnp.sum(grad_hidden_one * normed_one, axis=0),
        jnp.sum(grad_hidden_one, axis=0),
        jnp.sum(wide(grad_query), axis=0),
        jnp.sum(wide(grad_values), axis=0),
        jnp.sum(grad_second, axis=0),
        jnp.sum(grad_hidden_two * normed_two, axis=0),
        jnp.sum(grad_hidden_two, axis=0),
        jnp.sum(wide(upstream), axis=0),
    ] + [jnp.sum(item, axis=0) for item in grad_inner]
    vec_grad = jnp.stack(sums + [jnp.zeros_like(sums[0])] * BLOCKS)
    sum_attn, vec_sum = reduce_all(
        n_seq, n_fsdp, [item.astype(LOW) for item in squares], vec_grad
    )
    attn = wide(sum_attn)
    inner_grad = (
        sum_inner.reshape(BLOCKS, depth, n_fsdp, depth)
        .transpose(1, 2, 0, 3)
        .reshape(depth, n_fsdp, BLOCKS * depth)[:, :, :ff_own]
        .reshape(inner_weight.shape)
        .astype(WIDE)
    )
    outer_grad = wide(sum_outer.reshape(BLOCKS * depth, width)[:ff_own])
    return (
        layer_out.reshape(count, block_len, width),
        images_grad.reshape(count, block_len, width),
        vec_sum[0],
        vec_sum[1],
        attn[0],
        attn[1],
        attn[2],
        vec_sum[2],
        vec_sum[3],
        attn[3],
        vec_sum[4],
        vec_sum[5],
        vec_sum[6],
        inner_grad,
        vec_sum[8 : 8 + BLOCKS].reshape(BLOCKS * depth)[:ff_own],
        outer_grad,
        vec_sum[7],
    )


def solution(mesh):
    vector, matrix, tokens = P("fsdp"), P("fsdp", None), P("fsdp", "seq", None)
    params = (
        vector,
        vector,
        matrix,
        matrix,
        matrix,
        vector,
        vector,
        matrix,
        vector,
        vector,
        vector,
        matrix,
        vector,
        matrix,
        vector,
    )
    return jax.shard_map(
        functools.partial(shards, mesh.shape["seq"], mesh.shape["fsdp"]),
        mesh=mesh,
        in_specs=(tokens, matrix) + params + (tokens,),
        out_specs=(tokens, tokens) + params,
        check_vma=False,
    )
```

time: 1210 us -> 607 us (0.50)
  blocking collectives: 529 us -> 0 us
  Pallas kernels: 0 us -> 441 us
  waiting for transfers between devices: 355 us -> 0 us
  local copies, waits for them, and re-layouts: 111 us -> 49.4 us
  matrix products: 148 us -> 89.5 us
  starting transfers between devices: 22.1 us -> 0 us
  between operations: 18.5 us -> 1.26 us
    unnamed x3 -> x0, blocking collectives: 450 us -> none
    pallas_call x0 -> x3, Pallas kernels: none -> 441 us  [the longest x1 185 us: forward_all(): pl.pallas_call(functools.partial(forward_kernel, n_seq, n_fsdp, packs), o...]
    all_gather x6 -> x0, waiting for transfers between devices: 166 us -> none  [the longest x1 72.6 us: shards(): lax.all_gather(inner_weight, 'fsdp', axis=0, tiled=True)]
    psum x1 -> x0, waiting for transfers between devices: 91.7 us -> none  [shards(): lax.psum((shard_grads[0], shard_grads[1], shard_grads[2], shard_grads[3],...]
    all_to_all x3 -> x0, blocking collectives: 62.3 us -> none  [the longest x1 21.9 us: shards(): lax.all_to_all(grad_key_heads, 'seq', split_axis=1, concat_axis=2, tiled=...]
    dot_general x27 -> x9, matrix products: 69 us -> 19.8 us  [product(): return jnp.dot(left, right, preferred_element_type=WIDE)]
    all_to_all x5 -> x0, waiting for transfers between devices: 47.7 us -> none  [the longest x1 18.1 us: shards(): lax.all_to_all(grad_query_heads, 'seq', split_axis=1, concat_axis=2, tile...]
    reduce_scatter x5 -> x0, waiting for transfers between devices: 45.7 us -> none  [the longest x1 45.6 us: shards(): lax.psum_scatter(mlp_terms[2], 'fsdp', scatter_dimension=0, tiled=True)]
  transfers between devices with their start and end apart: 18 -> 0, of which waited for: 10 -> 0; matrix products, arithmetic and copies ran while one was open for 51% -> 0% of each run, Pallas kernels for 0% -> 0%
where the time goes in v2:
time: 607 us; the launch traced here: 597 us
  Pallas kernels  441 us (73%)
  matrix products  89.5 us (15%)
  local copies, waits for them, and re-layouts  49.4 us (8%)
  other arithmetic  15.7 us (3%)
    pallas_call x1, Pallas kernels, forward_all(): pl.pallas_call(functools.partial(forward_kernel, n_seq, n_fsdp, packs), o...  185 us
    pallas_call x1, Pallas kernels, backward_all(): pl.pallas_call(functools.partial(backward_kernel, n_seq, n_fsdp, packs),...  173 us
    pallas_call x1, Pallas kernels, reduce_all(): pl.pallas_call(functools.partial(reduce_kernel, n_seq, n_fsdp, packs), ou...  82.9 us
    dot_general x12, matrix products, product_rows(): lax.dot_general(left, right, (((0,), (0,)), ((), ())), preferred_element_...  41 us
    dot_general x12, matrix products, product_back(): lax.dot_general(left, right, (((1,), (1,)), ((), ())), preferred_element_...  28.7 us
    dot_general x9, matrix products, product(): return jnp.dot(left, right, preferred_element_type=WIDE)  19.8 us

profile of v2, /device:TPU:0, one launch (start us, length us, event | category | flops | bytes accessed | tf_op | source)
XLA Modules:
  0.0 596.8 jit_solution(14929365862933967992)
XLA Ops:
  16.8 2.8 reshape.170
  19.6 2.0 copy.35
  21.6 2.9 reshape.171.refs_4_
  24.5 185.4 %forward_attention.1 = (bf16[4,1152,1152]{2,1,0:T(8,128)(2,1)}, bf16[4,1152,1152]{2,1,0:T(8,128)(2,1)}, bf16[4,1152,1152]{2,1,0:T(8,128)(2,1)}, f32[16,1152]{1,0...) custom-call(bf16[3,128,1152]{2,1,0:T(8,128)(2,1)} %refs_0_.1, ...), custom_call_target="tpu_custom_call" | custom-call | tf_op jit(solution)/shard_map/forward_attention/pallas_call | solution.py:368
  211.0 3.6 fusion.106
  215.4 3.5 convolution_add_fusion.6
  227.7 2.0 fusion.108
  231.6 2.0 fusion.107
  240.6 4.2 convolution_convert_fusion.12.refs_8_
  244.8 3.2 convolution_convert_fusion.refs_3_
  248.0 3.4 convolution_convert_fusion.4.refs_7_
  251.4 3.2 convolution_convert_fusion.5.refs_6_
  254.5 3.2 convolution_convert_fusion.6.refs_5_
  257.7 3.2 convolution_convert_fusion.7.refs_4_
  266.0 2.9 fusion.2
  268.9 3.6 convolution_convert_fusion.8.refs_3_
  272.5 3.3 convolution_convert_fusion.9.refs_2_
  275.8 3.4 convolution_convert_fusion.10.refs_1_
  279.2 3.4 convolution_convert_fusion.11.refs_0_
  282.6 172.8 %backward_attention.1 = (bf16[4,144,1152]{2,1,0:T(8,128)(2,1)}, bf16[4,144,1152]{2,1,0:T(8,128)(2,1)}, bf16[3,384,1152]{2,1,0:T(8,128)(2,1)}) custom-call(bf16[1152,1152]{1,0:T(8,128)(2,1)} %convolution_convert_fusion.11.refs_0_, bf16[1152,1152]{1,0:T(8,128)(2,1)} %convolution_convert_fusion.10.refs_1_, ...), custom_call_target="tpu_custom_call" | custom-call | tf_op jit(solution)/shard_map/backward_attention/pallas_call | solution.py:692
  457.1 5.4 reshape.176
  462.6 6.1 %copy.40 = bf16[4,144,8,144]{3,0,2,1:T(4,128)(2,1)} copy(bf16[4,144,8,144]{3,2,1,0:T(8,128)(2,1)} %reshape.176) | data formatting | bytes 2654208 | tf_op jit(solution)/shard_map/reshape | solution.py:945
  468.7 5.0 reshape.177
  473.6 3.0 slice_convert_fusion.1
  478.4 4.4 reshape.181
  482.8 3.6 fusion.5
  486.5 3.2 convolution_add_fusion.1
  489.7 3.6 multiply_reduce_fusion.1
  496.5 4.8 convolution_convert_fusion.3.refs_0_
  501.3 3.2 convolution_convert_fusion.1.refs_2_
  504.5 3.2 convolution_convert_fusion.2.refs_1_
  507.7 82.9 %reduce_grads.1 = (bf16[4,144,1152]{2,1,0:T(8,128)(2,1)}, f32[16,144]{1,0:T(8,128)}) custom-call(bf16[1152,1152]{1,0:T(8,128)(2,1)} %convolution_convert_fusion.3.refs_0_, bf16[1152,1152]{1,0:T(8,128)(2,1)} %convolution_convert_fusion.2.refs_1_, bf16[1152,1152]{1,0:T(8,128)(2,1)} %convolution_convert_fusion.1.refs_2_, ...), custom_call_target="tpu_custom_call" | custom-call | tf_op jit(solution)/shard_map/reduce_grads/pallas_call | solution.py:799
  (106 shorter events, 53.3 us)
Async XLA Ops:
  0.7 9.8 %copy-start.2 = (bf16[3,128,1152]{2,1,0:T(8,128)(2,1)S(1)}, bf16[3,128,1152]{2,1,0:T(8,128)(2,1)}, u32[]{:S(2)}) copy-start(bf16[3,128,1152]{2,1,0:T(8,128)(2,1)} %param.35) | copy-start | bytes 2654212
  0.7 8.4 %copy-start.13 = (bf16[538]{0:T(1024)(128)(2,1)S(1)}, bf16[538]{0:T(1024)(128)(2,1)}, u32[]{:S(2)}) copy-start(bf16[538]{0:T(1024)(128)(2,1)} %param.32) | copy-start | bytes 3232
  0.7 9.7 %copy-start.12 = (s32[3,512]{1,0:T(4,128)S(1)}, s32[3,512]{1,0:T(4,128)}, u32[]{:S(2)}) copy-start(s32[3,512]{1,0:T(4,128)} %param.19) | copy-start | bytes 18436
  6.0 5.7 copy-start.8
  6.0 5.7 copy-start.9
  6.0 5.7 copy-start.10
  6.0 5.7 copy-start.11
  10.6 2.5 copy-start.4
  13.0 1.8 copy-start.5
  24.5 186.5 %copy-start = (bf16[3,128,1152]{2,1,0:T(8,128)(2,1)S(1)}, bf16[3,128,1152]{2,1,0:T(8,128)(2,1)}, u32[]{:S(2)}) copy-start(bf16[3,128,1152]{2,1,0:T(8,128)(2,1)} %refs_0_.1) | copy-start | bytes 2654212
  214.6 4.8 copy-start.14
  215.3 4.4 copy-start.3
  215.3 6.4 %slice-start = ((s8[10616832]{0:T(1024)(128)(4,1)}), s8[4194304]{0:T(1024)(128)(4,1)S(1)}, s32[]{:S(2)}) async-start(s8[10616832]{0:T(1024)(128)(4,1)} %bitcast.218), calls=%async_computation | async-start | bytes 8388608
  219.8 2.5 slice-start.1
  219.8 3.2 slice-start.2
  240.6 4.2 copy-start.16
  473.6 3.0 copy-start.1
  482.8 3.6 copy-start.6
  496.5 4.8 copy-start.7
  496.5 4.8 copy-start.15

commit v3 on v2

v3 whole, which is shorter than its diff:
```python
import functools

import jax
import jax.numpy as jnp
from jax import lax
from jax.experimental import pallas as pl
from jax.experimental.pallas import tpu as pltpu
from jax.sharding import PartitionSpec as P

HD = 72
EPSILON = 1e-06
MASKED = -1e30
LOG2_E = 1.4426950408889634
MESH = pl.DeviceIdType.MESH
VMEM_LIMIT = 67_000_000
BLOCKS = 4
LOW = jnp.bfloat16
WIDE = jnp.float32


def wide(values):
    return values.astype(WIDE)


def product(left, right):
    return jnp.dot(left, right, preferred_element_type=WIDE)


def product_rows(left, right):
    return lax.dot_general(left, right, (((0,), (0,)), ((), ())), preferred_element_type=WIDE)


def product_back(left, right):
    return lax.dot_general(left, right, (((1,), (1,)), ((), ())), preferred_element_type=WIDE)


def flip(index, bit):
    on = lax.rem(lax.div(index, 1 << bit), 2)
    return index + (1 - 2 * on) * (1 << bit)


def flip_mask(index, mask):
    bit = 0
    while mask >> bit:
        if (mask >> bit) & 1:
            index = flip(index, bit)
        bit += 1
    return index


PLAN = (((0, (0,), 0), (1, (0, 1), 1)), ((1, (0,), 0), (0, (0, 2), 1)))


class Place:
    def __init__(self, n_seq, n_fsdp, depth):
        self.n_seq, self.n_fsdp, self.depth = n_seq, n_fsdp, depth
        self.n_z = n_fsdp // 2
        self.s, self.f = lax.axis_index("seq"), lax.axis_index("fsdp")
        self.core, self.z = lax.rem(self.f, 2), lax.div(self.f, 2)
        self.block = lax.rem(self.s, BLOCKS)
        self.other = self.f + 1 - 2 * self.core
        n_z = self.n_z
        self.to_f = [lax.rem(self.z + d, n_z) * 2 + self.core for d in range(n_z)]
        self.from_f = [lax.rem(self.z - d + n_z, n_z) * 2 + self.core for d in range(n_z)]
        self.to_s = [lax.rem(self.s + d, n_seq) for d in range(n_seq)]
        self.from_s = [lax.rem(self.s - d + n_seq, n_seq) for d in range(n_seq)]
        first = depth // 32 * 16
        self.halves = ((0, first), (first, depth - first))
        self.sent = []

    def greet(self):
        barrier = pltpu.get_barrier_semaphore()
        peers = [(self.s, self.other)]
        peers += [(self.s, f) for f in self.to_f[1:]]
        peers += [(s, self.f) for s in self.to_s[1:]]
        for s, f in peers:
            pl.semaphore_signal(
                barrier, inc=1, device_id={"seq": s, "fsdp": f}, device_id_type=MESH
            )
        pl.semaphore_wait(barrier, len(peers))

    def copy(self, src, dst, sems, index, s, f):
        return pltpu.make_async_remote_copy(
            src_ref=src,
            dst_ref=dst,
            send_sem=sems[0].at[index],
            recv_sem=sems[1].at[index],
            device_id={"seq": s, "fsdp": f},
            device_id_type=MESH,
        )

    def start(self, copies):
        for copy in copies:
            copy.start()
            self.sent.append(copy)

    def finish(self):
        for copy in self.sent:
            copy.wait_send()

    def rows(self, f, half=None):
        offset, size = (0, self.depth) if half is None else self.halves[half]
        return pl.ds(pl.multiple_of(f * self.depth + offset, 8), size)

    def part(self, half):
        return pl.ds(*self.halves[half])


def arrive(copies):
    for copy in copies:
        copy.wait_recv()


class Exchange:
    def __init__(self, place, out, into, sems, local):
        self.place, self.out, self.into, self.sems, self.local = place, out, into, sems, local

    def send(self, i):
        at = self.place
        at.start(
            at.copy(
                self.out.at[i, at.to_s[d]],
                self.into.at[i, at.s],
                self.sems,
                (i, d),
                at.to_s[d],
                at.f,
            )
            for d in range(1, at.n_seq)
        )
        self.keep(i).start()

    def keep(self, i):
        at = self.place
        return pltpu.make_async_copy(
            self.out.at[i, at.s], self.into.at[i, at.s], self.local.at[i]
        )

    def receive(self, i):
        at = self.place
        arrive(
            at.copy(
                self.out.at[i, at.to_s[d]],
                self.into.at[i, at.from_s[d]],
                self.sems,
                (i, d),
                at.to_s[d],
                at.f,
            )
            for d in range(1, at.n_seq)
        )
        self.keep(i).wait()


def heads_of(ref, w, head, n_seq):
    rows = slice(head * HD, (head + 1) * HD)
    return jnp.concatenate([ref[t, w, rows, :] for t in range(n_seq)], axis=1)


def normalize(values):
    center = values - jnp.mean(values, axis=-1, keepdims=True)
    factor = lax.rsqrt(jnp.mean(center * center, axis=-1, keepdims=True) + EPSILON)
    return (center * factor, factor)


def norm_back(grad_normed, normed, factor):
    first = jnp.mean(grad_normed, axis=-1, keepdims=True)
    second = jnp.mean(grad_normed * normed, axis=-1, keepdims=True)
    return factor * (grad_normed - first - normed * second)


GELU_SCALE = 0.7978845608028654
GELU_CUBE = 0.044715


def gelu(u):
    return 0.5 * u * (1.0 + jnp.tanh(GELU_SCALE * (u + GELU_CUBE * (u * u * u))))


def gelu_slope(u):
    square = u * u
    bent = jnp.tanh(GELU_SCALE * (u + GELU_CUBE * (u * square)))
    inner = GELU_SCALE * (1.0 + 3.0 * GELU_CUBE * square)
    return 0.5 * (1.0 + bent) + 0.5 * u * (1.0 - bent * bent) * inner


def row_loop(count, body, carry=0, step=16):
    step = step if count % step == 0 else 8
    return lax.fori_loop(
        0,
        count // step,
        lambda i, kept: body(pl.ds(pl.multiple_of(i * step, step), step), kept),
        carry,
    )


def fold(values):
    return sum(values[8 * i : 8 * i + 8] for i in range(values.shape[0] // 8))


def column_sum(kept):
    return jnp.sum(kept, axis=0, keepdims=True)


def tall_product(left, right, out):
    width = left.shape[1]
    tile = 384 if width % 384 == 0 else width

    def body(i, _):
        cols = pl.ds(pl.multiple_of(i * tile, 128), tile)
        out[cols, :] = product_rows(left[:, cols], right[...]).astype(LOW)
        return 0

    lax.fori_loop(0, width // tile, body, 0)


def pieces_to_columns(read, n_fsdp, size, width):
    parts = []
    for f in range(n_fsdp):
        piece = read(f)
        if size < width:
            piece = jnp.concatenate(
                [piece, jnp.zeros((piece.shape[0], width - size), piece.dtype)], axis=1
            )
        parts.append(piece)
    return jnp.concatenate(parts, axis=1)


def forward_heads(i, heads, n_seq, qkv, mask, logsum):
    scale = HD ** (-0.5) * LOG2_E
    outs, sums = [], []
    for h in range(heads):
        query, keys, values = (heads_of(qkv, w, h, n_seq) for w in range(3))
        scores = product_rows(keys, query) + mask[i]
        highest = jnp.max(scores, axis=0, keepdims=True)
        weights = jnp.exp2((scores - highest) * scale)
        total = jnp.sum(weights, axis=0, keepdims=True)
        outs.append(product(values, (weights * (1.0 / total)).astype(LOW)))
        sums.append(highest * scale + jnp.log2(total))
    logsum[i] = jnp.concatenate(sums, axis=0)
    return jnp.concatenate(outs, axis=0)


def backward_heads(i, heads, n_seq, qkv, attended, grad, mask, logsum):
    scale = HD ** (-0.5)
    grads = [[], [], []]
    for h in range(heads):
        query, keys, values = (heads_of(qkv, w, h, n_seq) for w in range(3))
        grad_out = heads_of(grad, 0, h, n_seq)
        delta = jnp.sum(
            wide(grad_out) * wide(heads_of(attended, 0, h, n_seq)), axis=0, keepdims=True
        )
        scores = product_rows(keys, query) * (scale * LOG2_E)
        chance = jnp.exp2(scores + mask[i] - logsum[i, h : h + 1, :])
        grad_scores = chance * (product_rows(values, grad_out) - delta) * scale
        grads[2].append(product_back(grad_out, chance.astype(LOW)))
        grad_scores = grad_scores.astype(LOW)
        grads[0].append(product(keys, grad_scores))
        grads[1].append(product_back(query, grad_scores))
    return [jnp.concatenate(item, axis=0) for item in grads]


def scatter_tokens(value, n_seq, out, i, w):
    block = value.shape[1] // n_seq
    low = value.astype(LOW)
    for t in range(n_seq):
        out[i, t, w] = low[:, t * block : (t + 1) * block]


def forward_kernel(n_seq, n_fsdp, packs, *refs):
    refs = list(refs)

    def take(n):
        items = refs[:n]
        del refs[:n]
        return items

    images, mask, vec, inner_own = take(4)
    own = take(packs - 1)
    full = take(packs)
    vec_rows, logsum = take(2)
    hidden_out, flat_out, second_out, hidden_two_out, inner_out, active_out = take(6)
    qkv_out, attended_out = take(2)
    weight, vec_full, spread, qkv, attended, attended_in = take(6)
    hidden, attended_flat, second, inner, active, inner_block = take(6)
    own.insert(1, inner_block)
    z_sems, p_sems, c_sems, v_sems, a_sems, b_sems = (take(2) for _ in range(6))
    local, load, a_local, b_local, o_sem, i_sem = take(6)
    rows_all, width = images.shape
    count, _, _, _, block = qkv.shape
    depth = own[0].shape[1]
    group = width // n_seq
    heads = group // HD
    at = Place(n_seq, n_fsdp, depth)
    n_z = at.n_z
    at.greet()

    def vec_copy(src, dst, sem, f):
        return at.copy(src, vec_full.at[dst], v_sems, sem, at.s, f)

    def z_copy(p, d, arriving):
        dst = full[p].at[at.block, at.rows(at.from_f[d] if arriving else at.f)]
        return at.copy(own[p].at[at.block], dst, z_sems, (p, d), at.s, at.to_f[d])

    def plane(p, d, k, arriving):
        for half, steps in enumerate(PLAN):
            bit, masks, slot = steps[k]
            rows = at.rows(at.from_f[d], half)
            for i, m in enumerate(masks):
                src = full[p].at[flip_mask(at.block, m), rows]
                dst = full[p].at[flip_mask(at.block, m ^ (1 << bit)), rows] if arriving else src
                yield at.copy(src, dst, p_sems, (p, d, half, slot + i), flip(at.s, bit), at.f)

    def core_copy(p, d, arriving):
        f = at.from_f[d]
        src = own[p] if d == 0 else full[p].at[:, at.rows(f)]
        dst = full[p].at[:, at.rows(f + 1 - 2 * at.core if arriving else f)]
        return at.copy(src, dst, c_sems, (p, d), at.s, at.other)

    at.start([vec_copy(vec, at.f, d, at.to_f[d]) for d in range(1, n_z)])
    at.start([vec_copy(vec, at.f, 0, at.other)])
    at.start([z_copy(0, d, False) for d in range(1, n_z)])
    ff_own = inner_own.shape[1] // n_fsdp

    def relayout(rows, _):
        values = inner_own[rows, :]
        for q in range(BLOCKS):
            size = min(depth, ff_own - q * depth)
            inner_block[q, rows, :] = pieces_to_columns(
                lambda f, q=q, size=size: values[
                    :, f * ff_own + q * depth : f * ff_own + q * depth + size
                ],
                n_fsdp,
                size,
                depth,
            )
        return 0

    row_loop(depth, relayout)
    at.start([z_copy(p, d, False) for p in range(1, packs) for d in range(1, n_z)])
    keep = [
        pltpu.make_async_copy(own[p], full[p].at[:, at.rows(at.f)], local.at[p])
        for p in range(packs)
    ] + [pltpu.make_async_copy(vec, vec_full.at[at.f], local.at[packs])]
    for copy in keep:
        copy.start()
    at.start([core_copy(p, 0, False) for p in range(packs)])
    for d in range(1, n_z):
        arrive([vec_copy(vec, at.from_f[d], d, at.to_f[d])])
        at.start([vec_copy(vec_full.at[at.from_f[d]], at.from_f[d], n_z - 1 + d, at.other)])
    for d in range(n_z):
        sem = n_z - 1 + d if d else 0
        f = at.from_f[d] + 1 - 2 * at.core
        arrive([vec_copy(vec_full.at[f], f, sem, at.other)])
    keep[packs].wait()

    vec_rows[...] = jnp.concatenate([wide(vec_full[f]) for f in range(n_fsdp)], axis=1)

    def first_norm(rows, _):
        normed, _ = normalize(wide(images[rows, :]))
        hidden[rows, :] = (normed * vec_rows[0:1, :] + vec_rows[1:2, :]).astype(LOW)
        return 0

    row_loop(rows_all, first_norm)

    def from_z(p, d):
        arrive([z_copy(p, d, True)])
        at.start(plane(p, d, 0, False))

    def second_step(p):
        for d in range(1, n_z):
            arrive(plane(p, d, 0, True))
            at.start(plane(p, d, 1, False))

    def to_core(p, d):
        arrive(plane(p, d, 1, True))
        at.start([core_copy(p, d, False)])

    def weight_load(w):
        return pltpu.make_async_copy(full[0].at[w], weight.at[w % 2], load.at[w % 2])

    send_heads = Exchange(at, spread, qkv, a_sems, a_local)
    send_tokens = Exchange(at, attended, attended_in, b_sems, b_local)

    for d in range(1, n_z):
        from_z(0, d)
    second_step(0)
    for d in range(1, n_z):
        from_z(1, d)
        to_core(0, d)
    for d in range(n_z):
        arrive([core_copy(0, d, True)])
    keep[0].wait()
    weight_load(0).start()
    for w in range(3):
        if w < 2:
            weight_load(w + 1).start()
        weight_load(w).wait()
        value = product(hidden[...], weight[w % 2])
        if w != 1:
            value = value + vec_rows[2 + w // 2 : 3 + w // 2, :]
        value = value.T.astype(LOW)
        for i in range(count):
            for t in range(n_seq):
                spread[i, t, w] = value[
                    t * group : (t + 1) * group, i * block : (i + 1) * block
                ]
    for i in range(count):
        send_heads.send(i)
    second_step(1)
    for d in range(1, n_z):
        from_z(2, d)
    for i in range(count):
        send_heads.receive(i)
        scatter_tokens(
            forward_heads(i, heads, n_seq, qkv.at[i], mask, logsum), n_seq, attended, i, 0
        )
        send_tokens.send(i)
        if i == 0:
            for d in range(1, n_z):
                to_core(1, d)
            second_step(2)
    saves = [
        pltpu.make_async_copy(qkv, qkv_out, o_sem.at[0]),
        pltpu.make_async_copy(attended, attended_out, o_sem.at[1]),
        pltpu.make_async_copy(hidden, hidden_out, o_sem.at[2]),
    ]
    for copy in saves:
        copy.start()

    def square_load(ref, q, slot):
        return pltpu.make_async_copy(ref.at[q], weight.at[slot], load.at[slot])

    square_load(full[0], 3, 0).start()
    keep[1].wait()
    for d in range(n_z):
        arrive([core_copy(1, d, True)])
    square_load(full[1], 0, 1).start()
    for i in range(count):
        send_tokens.receive(i)
        features = jnp.concatenate([attended_in[i, t, 0] for t in range(n_seq)], axis=0)
        attended_flat[i * block : (i + 1) * block, :] = wide(features).T.astype(LOW)

    square_load(full[0], 3, 0).wait()
    second[...] = product(attended_flat[...], weight[0])
    square_load(full[1], 1, 0).start()

    def second_norm(rows, _):
        value = wide(images[rows, :]) + second[rows, :] + vec_rows[4:5, :]
        second[rows, :] = value
        normed, _ = normalize(value)
        hidden[rows, :] = (normed * vec_rows[5:6, :] + vec_rows[6:7, :]).astype(LOW)
        return 0

    saves[2].wait()
    row_loop(rows_all, second_norm)
    more = [
        pltpu.make_async_copy(attended_flat, flat_out, o_sem.at[3]),
        pltpu.make_async_copy(second, second_out, o_sem.at[4]),
        pltpu.make_async_copy(hidden, hidden_two_out, o_sem.at[5]),
    ]
    for copy in more:
        copy.start()

    def inner_saves(q):
        slot = q % 2
        return [
            pltpu.make_async_copy(inner.at[slot], inner_out.at[q], i_sem.at[0, slot]),
            pltpu.make_async_copy(active.at[slot], active_out.at[q], i_sem.at[1, slot]),
        ]

    for q in range(BLOCKS):
        slot = q % 2
        if q >= 2:
            for copy in inner_saves(q - 2):
                copy.wait()
        square_load(full[1], q, 1 - slot).wait()
        inner[slot] = product(hidden[...], weight[1 - slot])
        if q + 2 < BLOCKS:
            square_load(full[1], q + 2, 1 - slot).start()

        def bend(rows, _, q=q, slot=slot):
            value = inner[slot, rows, :] + vec_rows[8 + q : 9 + q, :]
            inner[slot, rows, :] = value
            active[slot, rows, :] = gelu(value).astype(LOW)
            return 0

        row_loop(rows_all, bend)
        for copy in inner_saves(q):
            copy.start()
        if q + 1 < n_z:
            to_core(2, q + 1)
    for d in range(BLOCKS + 1, n_z):
        to_core(2, d)
    for q in (BLOCKS - 2, BLOCKS - 1):
        for copy in inner_saves(q):
            copy.wait()
    keep[2].wait()
    for d in range(n_z):
        arrive([core_copy(2, d, True)])
    for copy in saves[:2] + more:
        copy.wait()
    at.finish()


def spaces():
    return pl.BlockSpec(memory_space=pl.ANY), pl.BlockSpec(memory_space=pltpu.VMEM)


def pair(*dims):
    return [pltpu.SemaphoreType.DMA(dims), pltpu.SemaphoreType.DMA(dims)]


def forward_all(n_seq, n_fsdp, count, images, mask, vec, inner_weight, attn, outer):
    packs = 3
    rows, width = images.shape
    depth = width // n_fsdp
    length = mask.shape[1]
    n_z, group, block = n_fsdp // 2, width // n_seq, rows // count
    heads = group // HD
    dma, vmem, shape = pltpu.SemaphoreType.DMA, pltpu.VMEM, jax.ShapeDtypeStruct
    any_space, in_vmem = spaces()
    qkv = (count, n_seq, 3, group, block)
    att = (count, n_seq, 1, group, block)
    flat = (rows, width)
    return pl.pallas_call(
        functools.partial(forward_kernel, n_seq, n_fsdp, packs),
        out_shape=[shape((BLOCKS, width, width), LOW) for _ in range(packs)]
        + [
            shape((vec.shape[0], width), WIDE),
            shape((count, heads, length), WIDE),
            shape(flat, LOW),
            shape(flat, LOW),
            shape(flat, WIDE),
            shape(flat, LOW),
            shape((BLOCKS,) + flat, WIDE),
            shape((BLOCKS,) + flat, LOW),
            shape(qkv, LOW),
            shape(att, LOW),
        ],
        in_specs=[in_vmem] * 6,
        out_specs=[any_space] * packs + [in_vmem] * 2 + [any_space] * 8,
        scratch_shapes=[
            vmem((2, width, width), LOW),
            vmem((n_fsdp,) + vec.shape, LOW),
            vmem(qkv, LOW),
            vmem(qkv, LOW),
            vmem(att, LOW),
            vmem(att, LOW),
            vmem(flat, LOW),
            vmem(flat, LOW),
            vmem(flat, WIDE),
            vmem((2,) + flat, WIDE),
            vmem((2,) + flat, LOW),
            vmem((BLOCKS, depth, width), LOW),
            *pair(packs, n_z),
            *pair(packs, n_z, 2, BLOCKS - 1),
            *pair(packs, n_z),
            *pair(2 * n_z - 1),
            *pair(count, n_seq),
            *pair(count, n_seq),
            dma((packs + 1,)),
            dma((2,)),
            dma((count,)),
            dma((count,)),
            dma((6,)),
            dma((2, 2)),
        ],
        compiler_params=pltpu.CompilerParams(
            collective_id=0, has_side_effects=True, vmem_limit_bytes=VMEM_LIMIT
        ),
        name="forward_layer",
    )(images, mask, vec, inner_weight, attn, outer)


def add_rows(target, left, right, start, size):
    step = 16 if start % 16 == 0 and size % 16 == 0 else 8

    def body(i, _):
        rows = pl.ds(pl.multiple_of(start + i * step, step), step)
        target[rows, :] = (wide(left[rows, :]) + wide(right[rows, :])).astype(LOW)
        return 0

    lax.fori_loop(0, size // step, body, 0)


class Reduction:
    RING = 4
    Z_RING = 6

    @classmethod
    def scratch(cls, n_seq, n_fsdp, packs, depth, width):
        n_z, upper = n_fsdp // 2, n_seq.bit_length() - 3
        dma, vmem, ring = pltpu.SemaphoreType.DMA, pltpu.VMEM, cls.RING
        piece = (depth, width)
        return [
            vmem((ring, BLOCKS) + piece, LOW),
            vmem((ring, BLOCKS) + piece, LOW),
            vmem((ring, BLOCKS - 1) + piece, LOW),
            vmem((cls.Z_RING,) + piece, LOW),
            vmem((packs, n_z) + piece, LOW),
            vmem((packs, BLOCKS) + piece, LOW),
            vmem((max(upper, 1), ring, BLOCKS) + (piece if upper else (16, 128)), LOW),
            dma((ring,)),
            *pair(ring),
            *pair(ring, 2, BLOCKS - 1),
            *pair(packs, n_z),
            *pair(packs, 2, BLOCKS - 1),
            *pair(max(upper, 1), ring),
            pltpu.SemaphoreType.REGULAR((3 + max(upper, 1),)),
        ]

    def __init__(self, at, packs, grads, scratch):
        self.at, self.packs, self.grads = at, packs, grads
        (
            self.held,
            self.core_in,
            self.plane_in,
            self.z_out,
            self.z_in,
            self.total,
            self.upper_in,
            self.load_sem,
            *sems,
            self.credit,
        ) = scratch
        self.c_sems, self.p_sems, self.z_sems, self.g_sems, self.u_sems = (
            sems[2 * i : 2 * i + 2] for i in range(5)
        )
        self.upper = at.n_seq.bit_length() - 3
        self.count = packs * at.n_z
        self.flight = {}
        self.z_flight = []

    def where(self, i):
        p, t = divmod(i, self.at.n_z)
        return p, t, lax.rem(self.at.z + t + 1, self.at.n_z), i % self.RING

    def give(self, kind, s, f):
        pl.semaphore_signal(
            self.credit.at[kind], inc=1, device_id={"seq": s, "fsdp": f}, device_id_type=MESH
        )

    def need(self, i, kind):
        if i >= self.RING:
            pl.semaphore_wait(self.credit.at[kind], 1)

    def load(self, i):
        p, _, z, slot = self.where(i)
        rows = self.at.rows(2 * z + self.at.core)
        return pltpu.make_async_copy(
            self.grads[p].at[:, rows], self.held.at[slot], self.load_sem.at[slot]
        )

    def to_partner(self, i):
        p, _, z, slot = self.where(i)
        at = self.at
        rows = at.rows(2 * z + 1 - at.core)
        return at.copy(
            self.grads[p].at[:, rows], self.core_in.at[slot], self.c_sems, slot, at.s, at.other
        )

    def start(self, i):
        if i >= self.RING:
            for copy in self.flight.pop(i - self.RING):
                copy.wait_send()
        self.need(i, 0)
        self.flight[i] = []
        self.go(i, [self.to_partner(i)])
        self.load(i).start()

    def go(self, i, copies):
        for copy in copies:
            copy.start()
            self.flight[i].append(copy)

    def plane(self, i, k):
        at = self.at
        slot = i % self.RING
        for half, steps in enumerate(PLAN):
            bit, masks, first = steps[k]
            for j, m in enumerate(masks):
                src = self.held.at[slot, flip_mask(at.block, m ^ (1 << bit)), at.part(half)]
                dst = self.plane_in.at[slot, first + j, at.part(half)]
                yield at.copy(
                    src, dst, self.p_sems, (slot, half, first + j), flip(at.s, bit), at.f
                )

    def z_copy(self, i, number=0):
        p, t, z, _ = self.where(i)
        at = self.at
        return at.copy(
            self.z_out.at[number % self.Z_RING],
            self.z_in.at[p, t],
            self.z_sems,
            (p, t),
            at.s,
            2 * z + at.core,
        )

    def spread(self, p, k, arriving):
        at = self.at
        for half, steps in enumerate(PLAN):
            bit, masks, slot = steps[k]
            for i, m in enumerate(masks):
                src = self.total.at[p, flip_mask(at.block, m), at.part(half)]
                dst = self.total.at[p, flip_mask(at.block, m ^ (1 << bit)), at.part(half)]
                yield at.copy(
                    src,
                    dst if arriving else src,
                    self.g_sems,
                    (p, half, slot + i),
                    flip(at.s, bit),
                    at.f,
                )

    def add_all(self, slot, term):
        def body(q, _):
            held = self.held.at[slot, q]
            add_rows(held, held, term.at[q], 0, self.at.depth)
            return 0

        lax.fori_loop(0, BLOCKS, body, 0)

    def stage_core(self, i):
        at = self.at
        slot = i % self.RING
        more = i + self.RING < self.count
        self.load(i).wait()
        arrive([self.to_partner(i)])
        self.add_all(slot, self.core_in.at[slot])
        if more:
            self.give(0, at.s, at.other)
        for u in range(self.upper):
            peer = flip(at.s, 2 + u)
            self.need(i, 3 + u)
            copy = at.copy(
                self.held.at[slot], self.upper_in.at[u, slot], self.u_sems, (u, slot), peer, at.f
            )
            copy.start()
            copy.wait()
            self.add_all(slot, self.upper_in.at[u, slot])
            if more:
                self.give(3 + u, peer, at.f)
        self.need(i, 1)
        self.need(i, 2)
        self.go(i, self.plane(i, 1))

    def stage_plane(self, i, k):
        at = self.at
        p, t, _, slot = self.where(i)
        last = t == at.n_z - 1
        arrive(self.plane(i, k))
        number = len(self.z_flight)
        if k == 0 and not last and number >= self.Z_RING:
            self.z_flight[number - self.Z_RING].wait_send()
        for half, steps in enumerate(PLAN):
            _, masks, first = steps[k]
            for j, m in enumerate(masks):
                held = self.held.at[slot, flip_mask(at.block, m)]
                target = held
                if k == 0:
                    target = self.z_in.at[p, t] if last else self.z_out.at[number % self.Z_RING]
                add_rows(target, held, self.plane_in.at[slot, first + j], *at.halves[half])
        if k > 0:
            self.go(i, self.plane(i, k - 1))
            return
        if i + self.RING < self.count:
            for bit in range(2):
                self.give(1 + bit, flip(at.s, bit), at.f)
        if not last:
            copy = self.z_copy(i, number)
            copy.start()
            self.z_flight.append(copy)

    def stage_total(self, p):
        at = self.at
        last = at.n_z - 1
        arrive(self.z_copy(p * at.n_z + t) for t in range(last))

        def body(rows, _):
            value = wide(self.z_in[p, last, rows, :])
            for t in range(last):
                value = value + wide(self.z_in[p, t, rows, :])
            self.total[p, at.block, rows, :] = value.astype(LOW)
            return 0

        row_loop(at.depth, body)
        at.start(self.spread(p, 0, False))

    def stage_spread(self, p, k):
        arrive(self.spread(p, k - 1, True))
        if k < 2:
            self.at.start(self.spread(p, k, False))

    def events(self, i, time):
        return [
            (time, 0, functools.partial(self.stage_core, i)),
            (time + 1, 1, functools.partial(self.stage_plane, i, 1)),
            (time + 2, 2, functools.partial(self.stage_plane, i, 0)),
        ]

    def finish(self):
        for copies in self.flight.values():
            for copy in copies:
                copy.wait_send()
        for copy in self.z_flight[-self.Z_RING :]:
            copy.wait_send()


def backward_kernel(n_seq, n_fsdp, ff_own, *refs):
    refs = list(refs)

    def take(n):
        items = refs[:n]
        del refs[:n]
        return items

    packs = 3
    w_attn, w_inner, w_outer = take(3)
    inner_in, active_in, second_in, hidden_two_in, flat_in, hidden_one_in = take(6)
    images_in, cot_in, qkv_in, attended_in, mask, logsum, vecs = take(7)
    layer_out, images_grad, out_outer, out_attn, inner_grad, vec_out = take(6)
    grads = take(packs)
    square, op_one, op_two, act, low, inner, tmp, gs, back = take(9)
    qkv, attended, grad_spread, grad_heads, back_spread, back_in = take(6)
    vec_acc, sums, v_work, v_came, v_z = take(5)
    a_sems, b_sems, v_sems = take(2), take(2), take(2)
    a_local, b_local, s_sem, o_sem, act_sem, g_sem, h_sem, f_sem = take(8)
    rows_all, width = op_one.shape
    count, _, _, group, block = back_in.shape
    heads = group // HD
    depth = width // n_fsdp
    at = Place(n_seq, n_fsdp, depth)
    n_z, bits = at.n_z, n_seq.bit_length() - 1
    red = Reduction(at, packs, grads, refs)
    chunk = lambda p, t: p * n_z + t

    class Load:
        def __init__(self, target, sem):
            self.target, self.sem, self.copy = target, sem, None

        def start(self, src):
            self.copy = pltpu.make_async_copy(src, self.target, self.sem)
            self.copy.start()

        def wait(self):
            self.copy.wait()

    squares = [Load(square.at[k], s_sem.at[k]) for k in range(3)]
    ops = [Load(op_one, o_sem.at[0]), Load(op_two, o_sem.at[1])]
    acts = [Load(act.at[k], act_sem.at[k]) for k in range(2)]
    inners = Load(inner, f_sem.at[0])
    heads_in = [Load(qkv, h_sem.at[0]), Load(attended, h_sem.at[1])]
    stores = {}

    def store(key, src, dst, sem):
        stores[key] = pltpu.make_async_copy(src, dst, sem)
        stores[key].start()

    def stored(*keys):
        for key in keys:
            stores.pop(key).wait()

    send_heads = Exchange(at, grad_spread, grad_heads, a_sems, a_local)
    send_tokens = Exchange(at, back_spread, back_in, b_sems, b_local)

    ops[0].start(cot_in)
    acts[0].start(active_in.at[0])
    acts[1].start(active_in.at[1])
    ops[1].start(hidden_two_in)
    squares[2].start(w_outer.at[0])
    inners.start(inner_in.at[0])
    at.greet()
    ops[0].wait()

    for q in range(BLOCKS):
        acts[q % 2].wait()
        if q >= 2:
            stored(("outer", q - 2))
        tall_product(act.at[q % 2], op_one, square.at[q % 2])
        store(("outer", q), square.at[q % 2], grads[0].at[q], g_sem.at[0, q])
        if q + 2 < BLOCKS:
            acts[q % 2].start(active_in.at[q + 2])
    stored(("outer", BLOCKS - 2))
    squares[0].start(w_inner.at[0])
    stored(("outer", BLOCKS - 1))
    ops[1].wait()

    def mlp(q):
        more = q + 1 < BLOCKS
        squares[2].wait()
        tmp[...] = product_back(op_one[...], square[2])
        if more:
            squares[2].start(w_outer.at[q + 1])
        else:
            squares[2].start(w_attn.at[3])
        inners.wait()
        sums[0] = jnp.zeros_like(sums[0])

        def body(rows, _):
            value = tmp[rows, :] * gelu_slope(inner[rows, :])
            sums[0] += fold(value)
            low[rows, :] = value.astype(LOW)
            return 0

        row_loop(rows_all, body)
        vec_acc[8 + q : 9 + q, :] = column_sum(sums[0])
        inners.start(inner_in.at[q + 1] if more else second_in)
        squares[0].wait()
        if q == 0:
            gs[...] = product_back(low[...], square[0])
        else:
            gs[...] += product_back(low[...], square[0])
        if more:
            squares[0].start(w_inner.at[q + 1])
        if q > 0:
            stored(("inner", q - 1))
        tall_product(op_two, low, square.at[1])
        store(("inner", q), square.at[1], grads[1].at[q], g_sem.at[1, q])
        if not more:
            ops[1].start(flat_in)

    def second_norm():
        inners.wait()
        for k in range(4):
            sums[k] = jnp.zeros_like(sums[k])

        def body(rows, _):
            normed, factor = normalize(inner[rows, :])
            grad = gs[rows, :]
            up = wide(op_one[rows, :])
            value = up + norm_back(grad * vecs[5:6, :], normed, factor)
            gs[rows, :] = value
            low[rows, :] = value.astype(LOW)
            sums[0] += fold(grad * normed)
            sums[1] += fold(grad)
            sums[2] += fold(value)
            sums[3] += fold(up)
            return 0

        row_loop(rows_all, body)
        for k, row in enumerate((5, 6, 4, 7)):
            vec_acc[row : row + 1, :] = column_sum(sums[k])

    def attended_grad():
        squares[2].wait()
        tmp[...] = product_back(low[...], square[2])
        for i in range(count):
            value = tmp[i * block : (i + 1) * block, :].T.astype(LOW)
            for t in range(n_seq):
                grad_spread[i, t, 0] = value[t * group : (t + 1) * group]
            send_heads.send(i)
        heads_in[0].start(qkv_in.at[0])
        heads_in[1].start(attended_in.at[0])
        stored(("inner", BLOCKS - 1))

    def out_grad():
        ops[1].wait()
        tall_product(op_two, low, square.at[1])
        store(("attn", 3), square.at[1], grads[2].at[3], g_sem.at[2, 3])
        ops[1].start(hidden_one_in)

    def image(i):
        send_heads.receive(i)
        for copy in heads_in:
            copy.wait()
        for w, value in enumerate(
            backward_heads(i, heads, n_seq, qkv, attended, grad_heads.at[i], mask, logsum)
        ):
            scatter_tokens(value, n_seq, back_spread, i, w)
        send_tokens.send(i)
        if i + 1 < count:
            heads_in[0].start(qkv_in.at[i + 1])
            heads_in[1].start(attended_in.at[i + 1])

    def collect(i):
        send_tokens.receive(i)
        for w in range(3):
            features = jnp.concatenate([back_in[i, t, w] for t in range(n_seq)], axis=0)
            back[w, i * block : (i + 1) * block, :] = wide(features).T.astype(LOW)

    def attn_grads():
        ops[1].wait()
        for w in range(3):
            slot = (0, 2, 1)[w]
            if slot == 1:
                stored(("attn", 3))
            tall_product(op_two, back.at[w], square.at[slot])
            store(("attn", w), square.at[slot], grads[2].at[w], g_sem.at[2, w])
        acts[0].start(images_in)
        for w in range(3):
            stored(("attn", w))
            slot = (0, 2, 1)[w]
            squares[slot].start(w_attn.at[w])

    def input_grad():
        for w in range(3):
            slot = (0, 2, 1)[w]
            squares[slot].wait()
            value = product_back(back[w], square[slot])
            if w == 0:
                tmp[...] = value
            else:
                tmp[...] += value
            squares[slot].start(w_outer.at[w])
        acts[0].wait()
        for k in range(4):
            sums[k] = jnp.zeros_like(sums[k])

        def body(rows, _):
            normed, factor = normalize(wide(act[0, rows, :]))
            grad = tmp[rows, :]
            gs[rows, :] += norm_back(grad * vecs[0:1, :], normed, factor)
            sums[0] += fold(grad * normed)
            sums[1] += fold(grad)
            sums[2] += fold(wide(back[0, rows, :]))
            sums[3] += fold(wide(back[2, rows, :]))
            return 0

        row_loop(rows_all, body)
        for k in range(4):
            vec_acc[k : k + 1, :] = column_sum(sums[k])
        store("images", gs, images_grad, f_sem.at[1])
        at.start([vec_copy(0)])
        acts[0].start(active_in.at[0])
        acts[1].start(active_in.at[1])

    def output():
        for q in range(BLOCKS):
            slot = (0, 2, 1, 0)[q]
            squares[slot].wait()
            acts[q % 2].wait()
            inner[...] += product(act[q % 2], square[slot])
            if q == 0:
                squares[0].start(w_outer.at[BLOCKS - 1])
            if q + 2 < BLOCKS:
                acts[q % 2].start(active_in.at[q + 2])

        def body(rows, _):
            inner[rows, :] += vecs[7:8, :]
            return 0

        row_loop(rows_all, body)
        store("layer", inner, layer_out, f_sem.at[2])

    def vec_copy(i):
        src = vec_acc if i == 0 else v_work.at[i - 1]
        peer = (at.s, at.other) if i == 0 else (flip(at.s, i - 1), at.f)
        return at.copy(src, v_came.at[i], v_sems, i, *peer)

    def vec_z(d, arriving):
        z = lax.div(at.from_f[d], 2) if arriving else at.z
        return at.copy(v_work.at[bits], v_z.at[z], v_sems, bits + d, at.s, at.to_f[d])

    def vec_stage(i):
        arrive([vec_copy(i)])
        v_work[i] = (vec_acc[...] if i == 0 else v_work[i - 1]) + v_came[i]
        if i < bits:
            at.start([vec_copy(i + 1)])
        else:
            at.start([vec_z(d, False) for d in range(1, n_z)])

    def vec_last():
        arrive([vec_z(d, True) for d in range(1, n_z)])
        value = v_work[bits]
        for d in range(1, n_z):
            value = value + v_z[lax.div(at.from_f[d], 2)]
        for f in range(n_fsdp):

            @pl.when(at.f == f)
            def _(f=f):
                vec_out[...] = value[:, f * depth : (f + 1) * depth]

    def relayout():
        def body(rows, _):
            parts = []
            for f in range(n_fsdp):
                for q in range(BLOCKS):
                    size = min(depth, ff_own - q * depth)
                    parts.append((q, f * depth, size))
            values = [red.total[1, q, rows, :] for q in range(BLOCKS)]
            inner_grad[rows, :] = jnp.concatenate(
                [values[q][:, first : first + size] for q, first, size in parts], axis=1
            )
            return 0

        row_loop(depth, body)

    def save(p, out):
        store(("out", p), red.total.at[p], out, g_sem.at[p, BLOCKS])

    events = []

    def add(time, call, *args):
        events.append((time, 10, functools.partial(call, *args)))

    gap = 2.5
    first_attn = 2 * n_z + gap
    for i in range(2 * n_z):
        events += red.events(i, i)
        add(-1 if i < red.RING else i - 1.4 if i < n_z else max(i - 1.4, n_z - 0.3), red.start, i)
    for t in range(n_z):
        events += red.events(chunk(2, t), first_attn + t)
        add(first_attn - 0.3 if t < red.RING else first_attn + t - 1.4, red.start, chunk(2, t))
    for q in range(BLOCKS):
        add(q * n_z / BLOCKS * 0.9 + 0.5, mlp, q)
    add(n_z - 0.4, second_norm)
    add(n_z - 0.35, attended_grad)
    add(n_z + 0.5, out_grad)
    for i in range(count):
        add(n_z + 1.5 + i, image, i)
        add(max(n_z + 3.5 + i, first_attn - 1.4 + 0.1 * i), collect, i)
    add(first_attn - 0.4, attn_grads)
    add(first_attn + 0.5, input_grad)
    for i in range(bits + 1):
        add(first_attn + 1.2 + i, vec_stage, i)
    add(first_attn + bits + 2.5, vec_last)
    add(first_attn + 1.5, output)
    for p, last in enumerate((n_z + 1, 2 * n_z + 1, first_attn + n_z + 1)):
        add(last + 1.1, red.stage_total, p)
        add(last + 1.8, red.stage_spread, p, 1)
        add(last + 2.6, red.stage_spread, p, 2)
    add(n_z + 3.7, save, 0, out_outer)
    add(2 * n_z + 3.7, relayout)
    add(first_attn + n_z + 3.7, save, 2, out_attn)
    run_events(events)
    stored(*list(stores))
    red.finish()
    at.finish()


def run_events(events):
    for _, _, call in sorted(events, key=lambda e: e[:2]):
        call()


def backward_all(n_seq, n_fsdp, ff_own, weights, saved, images, cot, mask, logsum, vecs):
    inner, active, second, hidden_two, flat, hidden_one, qkv, attended = saved
    rows, width = images.shape
    depth, n_z, bits = width // n_fsdp, n_fsdp // 2, n_seq.bit_length() - 1
    count = qkv.shape[0]
    any_space, in_vmem = spaces()
    dma, vmem, shape = pltpu.SemaphoreType.DMA, pltpu.VMEM, jax.ShapeDtypeStruct
    tokens = (rows, width)
    square = (BLOCKS, width, width)
    return pl.pallas_call(
        functools.partial(backward_kernel, n_seq, n_fsdp, ff_own),
        out_shape=[
            shape(tokens, WIDE),
            shape(tokens, WIDE),
            shape((BLOCKS, depth, width), LOW),
            shape((BLOCKS, depth, width), LOW),
            shape((depth, n_fsdp * ff_own), LOW),
            shape((vecs.shape[0], depth), WIDE),
        ]
        + [shape(square, LOW) for _ in range(3)],
        in_specs=[any_space] * 13 + [in_vmem] * 3,
        out_specs=[any_space] * 4 + [in_vmem] * 2 + [any_space] * 3,
        scratch_shapes=[
            vmem((3, width, width), LOW),
            vmem(tokens, LOW),
            vmem(tokens, LOW),
            vmem((2,) + tokens, LOW),
            vmem(tokens, LOW),
            vmem(tokens, WIDE),
            vmem(tokens, WIDE),
            vmem(tokens, WIDE),
            vmem((3,) + tokens, LOW),
            vmem(qkv.shape[1:], LOW),
            vmem(attended.shape[1:], LOW),
            vmem(attended.shape, LOW),
            vmem(attended.shape, LOW),
            vmem(qkv.shape, LOW),
            vmem(qkv.shape, LOW),
            vmem(vecs.shape, WIDE),
            vmem((4, 8, width), WIDE),
            vmem((bits + 1,) + vecs.shape, WIDE),
            vmem((bits + 1,) + vecs.shape, WIDE),
            vmem((n_z,) + vecs.shape, WIDE),
            *pair(count, n_seq),
            *pair(count, n_seq),
            *pair(bits + n_z),
            dma((count,)),
            dma((count,)),
            dma((3,)),
            dma((2,)),
            dma((2,)),
            dma((3, BLOCKS + 1)),
            dma((2,)),
            dma((3,)),
            *Reduction.scratch(n_seq, n_fsdp, 3, depth, width),
        ],
        compiler_params=pltpu.CompilerParams(
            collective_id=1, has_side_effects=True, vmem_limit_bytes=VMEM_LIMIT
        ),
        name="backward_layer",
    )(
        *weights,
        inner,
        active,
        second,
        hidden_two,
        flat,
        hidden_one,
        images,
        cot,
        qkv,
        attended,
        mask,
        logsum,
        vecs,
    )


def shards(
    n_seq,
    n_fsdp,
    images,
    key_mask,
    attn_gain,
    attn_shift,
    query_weight,
    key_weight,
    value_weight,
    query_bias,
    value_bias,
    out_weight,
    out_bias,
    mlp_gain,
    mlp_shift,
    inner_weight,
    inner_bias,
    outer_weight,
    outer_bias,
    cotangent,
):
    count, block, width = images.shape
    rows = count * block
    depth = query_weight.shape[0]
    ff_own = outer_weight.shape[0]
    slack = BLOCKS * depth - ff_own
    small = [
        attn_gain,
        attn_shift,
        query_bias,
        value_bias,
        out_bias,
        mlp_gain,
        mlp_shift,
        outer_bias,
        jnp.pad(inner_bias, (0, slack + BLOCKS * depth)),
    ]
    vec = jnp.concatenate(small).reshape(16, depth)
    mask = jnp.where(key_mask > 0, 0.0, MASKED).astype(WIDE)[:, :, None]
    tokens = images.reshape(rows, width)
    forward = forward_all(
        n_seq,
        n_fsdp,
        count,
        tokens,
        mask,
        vec,
        inner_weight,
        jnp.stack((query_weight, key_weight, value_weight, out_weight)),
        jnp.pad(outer_weight, ((0, slack), (0, 0))).reshape(BLOCKS, depth, width),
    )
    weights, vecs, logsum = forward[:3], forward[3], forward[4]
    hidden_one, flat, second, hidden_two, inner, active, qkv, attended = forward[5:]
    layer_out, images_grad, outer_sum, attn_sum, inner_grad, vec_sum = backward_all(
        n_seq,
        n_fsdp,
        ff_own,
        weights,
        (inner, active, second, hidden_two, flat, hidden_one, qkv, attended),
        tokens,
        cotangent.reshape(rows, width),
        mask,
        logsum,
        vecs,
    )[:6]
    attn = wide(attn_sum)
    return (
        layer_out.reshape(count, block, width),
        images_grad.reshape(count, block, width),
        vec_sum[0],
        vec_sum[1],
        attn[0],
        attn[1],
        attn[2],
        vec_sum[2],
        vec_sum[3],
        attn[3],
        vec_sum[4],
        vec_sum[5],
        vec_sum[6],
        wide(inner_grad),
        vec_sum[8 : 8 + BLOCKS].reshape(BLOCKS * depth)[:ff_own],
        wide(outer_sum.reshape(BLOCKS * depth, width)[:ff_own]),
        vec_sum[7],
    )


def solution(mesh):
    vector, matrix, tokens = P("fsdp"), P("fsdp", None), P("fsdp", "seq", None)
    params = (
        vector,
        vector,
        matrix,
        matrix,
        matrix,
        vector,
        vector,
        matrix,
        vector,
        vector,
        vector,
        matrix,
        vector,
        matrix,
        vector,
    )
    return jax.shard_map(
        functools.partial(shards, mesh.shape["seq"], mesh.shape["fsdp"]),
        mesh=mesh,
        in_specs=(tokens, matrix) + params + (tokens,),
        out_specs=(tokens, tokens) + params,
        check_vma=False,
    )
```

time: 607 us -> 509 us (0.84)
  matrix products: 89.5 us -> 0 us
  local copies, waits for them, and re-layouts: 49.4 us -> 18.2 us
  Pallas kernels: 441 us -> 472 us
  other arithmetic: 15.7 us -> 8.06 us
    dot_general x33 -> x0, matrix products: 89.5 us -> none  [the longest x12 41 us: product_rows(): lax.dot_general(left, right, (((0,), (0,)), ((), ())), preferred_element_...]
    reshape x15 -> x1, local copies, waits for them, and re-layouts: 29.5 us -> 0.7 us  [shards(): vec = jnp.concatenate(small).reshape(16, depth)]
    pallas_call x1, Pallas kernels: 185 us -> 203 us  [forward_all(): pl.pallas_call(functools.partial(forward_kernel, n_seq, n_fsdp, packs), o...]
    pallas_call x2 -> x1, Pallas kernels: 256 us -> 269 us  [backward_all(): pl.pallas_call(functools.partial(backward_kernel, n_seq, n_fsdp, ff_own),...]
where the time goes in v3:
time: 509 us; the launch traced here: 500 us
  Pallas kernels  472 us (93%)
  local copies, waits for them, and re-layouts  18.2 us (4%)
  other arithmetic  8.06 us (2%)
    pallas_call x1, Pallas kernels, backward_all(): pl.pallas_call(functools.partial(backward_kernel, n_seq, n_fsdp, ff_own),...  269 us
    pallas_call x1, Pallas kernels, forward_all(): pl.pallas_call(functools.partial(forward_kernel, n_seq, n_fsdp, packs), o...  203 us

profile of v3, /device:TPU:0, one launch (start us, length us, event | category | flops | bytes accessed | tf_op | source)
XLA Modules:
  0.0 499.7 jit_solution(9976171778659891615)
XLA Ops:
  0.7 0.0 copy-start.3
  0.7 0.8 pad.8
  1.5 5.4 %concatenate.3 = bf16[2304]{0:T(1024)(128)(2,1)S(1)} concatenate(bf16[144]{0:T(256)(128)(2,1)} %param.20, bf16[144]{0:T(256)(128)(2,1)} %param.21, bf16[144]{0:T(256)(128)(2,1)} %param.25, bf16[144]{0:T(256)(128)(2,1)} %param.26, bf16[144]{0:T(256)(128)(2,1)} %param.28, bf16[144]{0:T(256)(128)(2,1)} %param.29, bf16[144]{0:T(256)(128)(2,1)} %param.30, bf16[144]{0:T(256)(128)(2,1)} %param.34, ...), dimensions={0} | concatenate | bytes 9216 | tf_op jit(solution)/shard_map/concatenate | solution.py:1254
  6.9 0.7 reshape.59.refs_2_
  7.6 0.7 select_bitcast_fusion
  8.3 1.2 copy.35.refs_1_.refs_13_
  9.5 2.5 pad_maximum_fusion.refs_4_
  12.0 0.0 copy-done.3
  12.0 1.2 pad.9
  13.2 203.1 %forward_layer.1 = (bf16[4,1152,1152]{2,1,0:T(8,128)(2,1)}, bf16[4,1152,1152]{2,1,0:T(8,128)(2,1)}, bf16[4,1152,1152]{2,1,0:T(8,128)(2,1)}, f32[16,1152]{1,0:T(8...) custom-call(bf16[384,1152]{1,0:T(8,128)(2,1)} %bitcast.30, ...), custom_call_target="tpu_custom_call" | custom-call | tf_op jit(solution)/shard_map/forward_layer/pallas_call | solution.py:526
  216.2 269.3 %backward_layer.1 = (f32[384,1152]{1,0:T(8,128)}, f32[384,1152]{1,0:T(8,128)}, bf16[4,144,1152]{2,1,0:T(8,128)(2,1)}, bf16[4,144,1152]{2,1,0:T(8,128)(2,1)}, bf1...) custom-call(bf16[4,1152,1152]{2,1,0:T(8,128)(2,1)} %get-tuple-elemen, ...), custom_call_target="tpu_custom_call" | custom-call | tf_op jit(solution)/shard_map/backward_layer/pallas_call | solution.py:1147
  485.5 0.7 slice.56
  486.2 1.6 fusion
  487.8 0.7 reshape.64
  488.5 0.0 copy-start.4
  488.5 3.0 convert_element_type.14
  491.5 0.0 copy-done.4
  491.5 0.0 copy-start.2
  491.5 1.6 slice_convert_fusion
  493.1 0.2 copy-done.2
  493.3 0.2 convert_element_type.13
  493.5 0.0 copy-start.1
  493.5 1.5 slice_bitcast_fusion
  495.1 0.9 copy-done.1
  496.0 0.0 copy-start
  496.0 1.2 copy.39
  497.2 0.9 copy-done
  498.1 1.2 copy.40
Async XLA Ops:
  0.7 11.3 %copy-start.3 = (bf16[538,1152]{1,0:T(8,128)(2,1)S(1)}, bf16[538,1152]{1,0:T(8,128)(2,1)}, u32[]{:S(2)}) copy-start(bf16[538,1152]{1,0:T(8,128)(2,1)} %param.33) | copy-start | bytes 3718660
  488.5 3.0 copy-start.4
  491.5 1.8 copy-start.2
  493.5 2.4 copy-start.1
  496.0 2.1 copy-start

commit v4 on v3

--- a/solution.py
+++ b/solution.py
@@ -60,10 +60,9 @@
         self.block = lax.rem(self.s, BLOCKS)
         self.other = self.f + 1 - 2 * self.core
         n_z = self.n_z
-        self.to_f = [lax.rem(self.z + d, n_z) * 2 + self.core for d in range(n_z)]
-        self.from_f = [lax.rem(self.z - d + n_z, n_z) * 2 + self.core for d in range(n_z)]
-        self.to_s = [lax.rem(self.s + d, n_seq) for d in range(n_seq)]
-        self.from_s = [lax.rem(self.s - d + n_seq, n_seq) for d in range(n_seq)]
+        self.across = [flip_mask(self.z, d) for d in range(n_z)]
+        self.to_f = self.from_f = [z * 2 + self.core for z in self.across]
+        self.to_s = self.from_s = [flip_mask(self.s, d) for d in range(n_seq)]
         first = depth // 32 * 16
         self.halves = ((0, first), (first, depth - first))
         self.sent = []
@@ -275,14 +274,14 @@
         del refs[:n]
         return items
 
-    images, mask, vec, inner_own = take(4)
+    images, mask, vec, inner_own, cot = take(5)
     own = take(packs - 1)
     full = take(packs)
     vec_rows, logsum = take(2)
-    hidden_out, flat_out, second_out, hidden_two_out, inner_out, active_out = take(6)
+    hidden_out, flat_out, second_out, hidden_two_out, inner_out, active_out, grad_out = take(7)
     qkv_out, attended_out = take(2)
     weight, vec_full, spread, qkv, attended, attended_in = take(6)
-    hidden, attended_flat, second, inner, active, inner_block = take(6)
+    hidden, attended_flat, second, inner, active, inner_block, stage = take(7)
     own.insert(1, inner_block)
     z_sems, p_sems, c_sems, v_sems, a_sems, b_sems = (take(2) for _ in range(6))
     local, load, a_local, b_local, o_sem, i_sem = take(6)
@@ -367,10 +366,9 @@
         arrive([z_copy(p, d, True)])
         at.start(plane(p, d, 0, False))
 
-    def second_step(p):
-        for d in range(1, n_z):
-            arrive(plane(p, d, 0, True))
-            at.start(plane(p, d, 1, False))
+    def second_step(p, d):
+        arrive(plane(p, d, 0, True))
+        at.start(plane(p, d, 1, False))
 
     def to_core(p, d):
         arrive(plane(p, d, 1, True))
@@ -382,12 +380,25 @@
     send_heads = Exchange(at, spread, qkv, a_sems, a_local)
     send_tokens = Exchange(at, attended, attended_in, b_sems, b_local)
 
-    for d in range(1, n_z):
-        from_z(0, d)
-    second_step(0)
-    for d in range(1, n_z):
-        from_z(1, d)
-        to_core(0, d)
+    def flow(p, shift):
+        for k in range(n_z + 1):
+            for late, step in enumerate((from_z, second_step, to_core)):
+                if 0 <= k - late < n_z - 1:
+                    yield k + shift, functools.partial(step, p, k - late + 1)
+
+    for _, step in list(flow(0, 0))[:-1]:
+        step()
+    later = sorted(list(flow(1, 0)) + list(flow(2, 2.6)), key=lambda item: item[0])
+    later = [step for _, step in later]
+    later.pop(0)()
+    to_core(0, n_z - 1)
+    cuts = [len(later) * k // 17 for k in (0, 4, 7, 11, 14, 16, 17)]
+    later = [later[a:b] for a, b in zip(cuts, cuts[1:])]
+
+    def go_on():
+        for step in later.pop(0) if later else ():
+            step()
+
     for d in range(n_z):
         arrive([core_copy(0, d, True)])
     keep[0].wait()
@@ -407,19 +418,14 @@
                 ]
     for i in range(count):
         send_heads.send(i)
-    second_step(1)
-    for d in range(1, n_z):
-        from_z(2, d)
+    go_on()
     for i in range(count):
         send_heads.receive(i)
         scatter_tokens(
             forward_heads(i, heads, n_seq, qkv.at[i], mask, logsum), n_seq, attended, i, 0
         )
         send_tokens.send(i)
-        if i == 0:
-            for d in range(1, n_z):
-                to_core(1, d)
-            second_step(2)
+        go_on()
     saves = [
         pltpu.make_async_copy(qkv, qkv_out, o_sem.at[0]),
         pltpu.make_async_copy(attended, attended_out, o_sem.at[1]),
@@ -467,6 +473,7 @@
         return [
             pltpu.make_async_copy(inner.at[slot], inner_out.at[q], i_sem.at[0, slot]),
             pltpu.make_async_copy(active.at[slot], active_out.at[q], i_sem.at[1, slot]),
+            pltpu.make_async_copy(stage.at[slot], grad_out.at[q], i_sem.at[2, slot]),
         ]
 
     for q in range(BLOCKS):
@@ -486,12 +493,11 @@
             return 0
 
         row_loop(rows_all, bend)
+        tall_product(active.at[slot], cot, stage.at[slot])
         for copy in inner_saves(q):
             copy.start()
-        if q + 1 < n_z:
-            to_core(2, q + 1)
-    for d in range(BLOCKS + 1, n_z):
-        to_core(2, d)
+        if q < BLOCKS - 1:
+            go_on()
     for q in (BLOCKS - 2, BLOCKS - 1):
         for copy in inner_saves(q):
             copy.wait()
@@ -511,7 +517,7 @@
     return [pltpu.SemaphoreType.DMA(dims), pltpu.SemaphoreType.DMA(dims)]
 
 
-def forward_all(n_seq, n_fsdp, count, images, mask, vec, inner_weight, attn, outer):
+def forward_all(n_seq, n_fsdp, count, images, mask, vec, inner_weight, cot, attn, outer):
     packs = 3
     rows, width = images.shape
     depth = width // n_fsdp
@@ -535,11 +541,12 @@
             shape(flat, LOW),
             shape((BLOCKS,) + flat, WIDE),
             shape((BLOCKS,) + flat, LOW),
+            shape((BLOCKS, width, width), LOW),
             shape(qkv, LOW),
             shape(att, LOW),
         ],
-        in_specs=[in_vmem] * 6,
-        out_specs=[any_space] * packs + [in_vmem] * 2 + [any_space] * 8,
+        in_specs=[in_vmem] * 7,
+        out_specs=[any_space] * packs + [in_vmem] * 2 + [any_space] * 9,
         scratch_shapes=[
             vmem((2, width, width), LOW),
             vmem((n_fsdp,) + vec.shape, LOW),
@@ -553,6 +560,7 @@
             vmem((2,) + flat, WIDE),
             vmem((2,) + flat, LOW),
             vmem((BLOCKS, depth, width), LOW),
+            vmem((2, width, width), LOW),
             *pair(packs, n_z),
             *pair(packs, n_z, 2, BLOCKS - 1),
             *pair(packs, n_z),
@@ -564,13 +572,13 @@
             dma((count,)),
             dma((count,)),
             dma((6,)),
-            dma((2, 2)),
+            dma((3, 2)),
         ],
         compiler_params=pltpu.CompilerParams(
             collective_id=0, has_side_effects=True, vmem_limit_bytes=VMEM_LIMIT
         ),
         name="forward_layer",
-    )(images, mask, vec, inner_weight, attn, outer)
+    )(images, mask, vec, inner_weight, cot, attn, outer)
 
 
 def add_rows(target, left, right, start, size):
@@ -634,7 +642,7 @@
 
     def where(self, i):
         p, t = divmod(i, self.at.n_z)
-        return p, t, lax.rem(self.at.z + t + 1, self.at.n_z), i % self.RING
+        return p, t, self.at.across[self.at.n_z - 1 - t], i % self.RING
 
     def give(self, kind, s, f):
         pl.semaphore_signal(
@@ -819,9 +827,9 @@
     packs = 3
     w_attn, w_inner, w_outer = take(3)
     inner_in, active_in, second_in, hidden_two_in, flat_in, hidden_one_in = take(6)
-    images_in, cot_in, qkv_in, attended_in, mask, logsum, vecs = take(7)
+    images_in, cot_in, grad_outer, qkv_in, attended_in, mask, logsum, vecs = take(8)
     layer_out, images_grad, out_outer, out_attn, inner_grad, vec_out = take(6)
-    grads = take(packs)
+    grads = [grad_outer] + take(packs - 1)
     square, op_one, op_two, act, low, inner, tmp, gs, back = take(9)
     qkv, attended, grad_spread, grad_heads, back_spread, back_in = take(6)
     vec_acc, sums, v_work, v_came, v_z = take(5)
@@ -866,29 +874,17 @@
     send_tokens = Exchange(at, back_spread, back_in, b_sems, b_local)
 
     ops[0].start(cot_in)
-    acts[0].start(active_in.at[0])
-    acts[1].start(active_in.at[1])
     ops[1].start(hidden_two_in)
     squares[2].start(w_outer.at[0])
+    squares[0].start(w_inner.at[0])
     inners.start(inner_in.at[0])
     at.greet()
-    ops[0].wait()
-
-    for q in range(BLOCKS):
-        acts[q % 2].wait()
-        if q >= 2:
-            stored(("outer", q - 2))
-        tall_product(act.at[q % 2], op_one, square.at[q % 2])
-        store(("outer", q), square.at[q % 2], grads[0].at[q], g_sem.at[0, q])
-        if q + 2 < BLOCKS:
-            acts[q % 2].start(active_in.at[q + 2])
-    stored(("outer", BLOCKS - 2))
-    squares[0].start(w_inner.at[0])
-    stored(("outer", BLOCKS - 1))
-    ops[1].wait()
 
     def mlp(q):
         more = q + 1 < BLOCKS
+        if q == 0:
+            for copy in ops:
+                copy.wait()
         squares[2].wait()
         tmp[...] = product_back(op_one[...], square[2])
         if more:
@@ -1118,11 +1114,12 @@
     add(first_attn + bits + 2.5, vec_last)
     add(first_attn + 1.5, output)
     for p, last in enumerate((n_z + 1, 2 * n_z + 1, first_attn + n_z + 1)):
-        add(last + 1.1, red.stage_total, p)
-        add(last + 1.8, red.stage_spread, p, 1)
-        add(last + 2.6, red.stage_spread, p, 2)
-    add(n_z + 3.7, save, 0, out_outer)
-    add(2 * n_z + 3.7, relayout)
+        late = 0 if p == packs - 1 else 2
+        add(last + late + 1.1, red.stage_total, p)
+        add(last + late + 1.8, red.stage_spread, p, 1)
+        add(last + late + 2.6, red.stage_spread, p, 2)
+    add(n_z + 5.7, save, 0, out_outer)
+    add(2 * n_z + 5.7, relayout)
     add(first_attn + n_z + 3.7, save, 2, out_attn)
     run_events(events)
     stored(*list(stores))
@@ -1136,7 +1133,7 @@
 
 
 def backward_all(n_seq, n_fsdp, ff_own, weights, saved, images, cot, mask, logsum, vecs):
-    inner, active, second, hidden_two, flat, hidden_one, qkv, attended = saved
+    inner, active, grad_outer, second, hidden_two, flat, hidden_one, qkv, attended = saved
     rows, width = images.shape
     depth, n_z, bits = width // n_fsdp, n_fsdp // 2, n_seq.bit_length() - 1
     count = qkv.shape[0]
@@ -1154,9 +1151,9 @@
             shape((depth, n_fsdp * ff_own), LOW),
             shape((vecs.shape[0], depth), WIDE),
         ]
-        + [shape(square, LOW) for _ in range(3)],
-        in_specs=[any_space] * 13 + [in_vmem] * 3,
-        out_specs=[any_space] * 4 + [in_vmem] * 2 + [any_space] * 3,
+        + [shape(square, LOW) for _ in range(2)],
+        in_specs=[any_space] * 14 + [in_vmem] * 3,
+        out_specs=[any_space] * 4 + [in_vmem] * 2 + [any_space] * 2,
         scratch_shapes=[
             vmem((3, width, width), LOW),
             vmem(tokens, LOW),
@@ -1205,6 +1202,7 @@
         hidden_one,
         images,
         cot,
+        grad_outer,
         qkv,
         attended,
         mask,
@@ -1249,9 +1247,11 @@
         mlp_gain,
         mlp_shift,
         outer_bias,
-        jnp.pad(inner_bias, (0, slack + BLOCKS * depth)),
     ]
-    vec = jnp.concatenate(small).reshape(16, depth)
+    vec = jnp.concatenate(
+        [item.reshape(1, depth) for item in small]
+        + [jnp.pad(inner_bias, (0, slack + BLOCKS * depth)).reshape(2 * BLOCKS, depth)]
+    )
     mask = jnp.where(key_mask > 0, 0.0, MASKED).astype(WIDE)[:, :, None]
     tokens = images.reshape(rows, width)
     forward = forward_all(
@@ -1262,17 +1262,18 @@
         mask,
         vec,
         inner_weight,
+        cotangent.reshape(rows, width),
         jnp.stack((query_weight, key_weight, value_weight, out_weight)),
         jnp.pad(outer_weight, ((0, slack), (0, 0))).reshape(BLOCKS, depth, width),
     )
     weights, vecs, logsum = forward[:3], forward[3], forward[4]
-    hidden_one, flat, second, hidden_two, inner, active, qkv, attended = forward[5:]
+    hidden_one, flat, second, hidden_two, inner, active, grad_outer, qkv, attended = forward[5:]
     layer_out, images_grad, outer_sum, attn_sum, inner_grad, vec_sum = backward_all(
         n_seq,
         n_fsdp,
         ff_own,
         weights,
-        (inner, active, second, hidden_two, flat, hidden_one, qkv, attended),
+        (inner, active, grad_outer, second, hidden_two, flat, hidden_one, qkv, attended),
         tokens,
         cotangent.reshape(rows, width),
         mask,

time: 509 us -> 478 us (0.939)
  Pallas kernels: 472 us -> 441 us
    pallas_call x1, Pallas kernels: 203 us -> 183 us  [forward_all(): pl.pallas_call(functools.partial(forward_kernel, n_seq, n_fsdp, packs), o...]
    pallas_call x1, Pallas kernels: 269 us -> 258 us  [backward_all(): pl.pallas_call(functools.partial(backward_kernel, n_seq, n_fsdp, ff_own),...]
where the time goes in v4:
time: 478 us; the launch traced here: 468 us
  Pallas kernels  441 us (92%)
  local copies, waits for them, and re-layouts  18.6 us (4%)
  other arithmetic  8.06 us (2%)
    pallas_call x1, Pallas kernels, backward_all(): pl.pallas_call(functools.partial(backward_kernel, n_seq, n_fsdp, ff_own),...  258 us
    pallas_call x1, Pallas kernels, forward_all(): pl.pallas_call(functools.partial(forward_kernel, n_seq, n_fsdp, packs), o...  183 us

profile of v4, /device:TPU:0, one launch (start us, length us, event | category | flops | bytes accessed | tf_op | source)
XLA Modules:
  0.0 468.5 jit_solution(2839279233187243316)
XLA Ops:
  0.7 0.0 copy-start.3
  0.7 0.8 reshape.84
  1.4 0.7 reshape.85
  2.1 0.7 reshape.86
  2.7 0.7 reshape.87
  3.4 0.7 reshape.88
  4.1 0.7 reshape.89
  4.7 0.7 reshape.90
  5.4 0.7 reshape.91
  6.0 0.7 pad.8
  6.7 0.1 reshape.92
  6.8 1.2 concatenate.3.refs_2_
  8.0 0.7 select_bitcast_fusion
  8.7 1.2 copy.35.refs_1_.refs_14_
  9.9 2.5 pad_maximum_fusion.refs_5_
  12.4 0.0 copy-done.3
  12.4 1.2 pad.9
  13.6 183.0 %forward_layer.1 = (bf16[4,1152,1152]{2,1,0:T(8,128)(2,1)}, bf16[4,1152,1152]{2,1,0:T(8,128)(2,1)}, bf16[4,1152,1152]{2,1,0:T(8,128)(2,1)}, f32[16,1152]{1,0:T(8...) custom-call(bf16[384,1152]{1,0:T(8,128)(2,1)} %bitcast.30, ...), custom_call_target="tpu_custom_call" | custom-call | tf_op jit(solution)/shard_map/forward_layer/pallas_call | solution.py:532
  196.6 257.6 %backward_layer.1 = (f32[384,1152]{1,0:T(8,128)}, f32[384,1152]{1,0:T(8,128)}, bf16[4,144,1152]{2,1,0:T(8,128)(2,1)}, bf16[4,144,1152]{2,1,0:T(8,128)(2,1)}, bf1...) custom-call(bf16[4,1152,1152]{2,1,0:T(8,128)(2,1)} %get-tuple-elemen, ...), custom_call_target="tpu_custom_call" | custom-call | tf_op jit(solution)/shard_map/backward_layer/pallas_call | solution.py:1144
  454.3 0.7 slice.56
  455.0 1.6 fusion
  456.6 0.7 reshape.97
  457.2 3.0 convert_element_type.14
  460.3 0.0 copy-done.4
  460.3 1.6 slice_convert_fusion
  461.9 0.2 copy-done.2
  462.1 0.2 convert_element_type.13
  462.3 1.5 slice_bitcast_fusion
  463.8 0.9 copy-done.1
  464.7 1.2 copy.39
  465.9 0.9 copy-done
  466.8 1.2 copy.40
  (4 shorter events, 0.0 us)
Async XLA Ops:
  0.7 11.8 %copy-start.3 = (bf16[538,1152]{1,0:T(8,128)(2,1)S(1)}, bf16[538,1152]{1,0:T(8,128)(2,1)}, u32[]{:S(2)}) copy-start(bf16[538,1152]{1,0:T(8,128)(2,1)} %param.33) | copy-start | bytes 3718660
  457.2 3.0 copy-start.4
  460.3 1.8 copy-start.2
  462.3 2.4 copy-start.1
  464.7 2.1 copy-start
